TPU v7x, 32 devices: a whole 2x2x4 slice. The times are simulated.
32 devices in a mesh: seq: 16 (over z, y, x), head: 2 (over core).
Axes of the slice: x: 2, y: 2, z: 4, core: 2. Of those that a mesh axis runs over, the one named last changes fastest.
Arguments:
- queries: bfloat16 [2048, 32, 128], P('seq', 'head'), may hold values from -6 to 6
- key_vectors: bfloat16 [2048, 32, 128], P('seq', 'head'), may hold values from -6 to 6
- values: bfloat16 [2048, 32, 128], P('seq', 'head'), may hold values from -6 to 6
- out_grad: bfloat16 [2048, 32, 128], P('seq', 'head'), may hold values from -6 to 6
- hidden_in: bfloat16 [2048, 2048], P('seq'), may hold values from -6 to 6
- decay_weight: bfloat16 [2048, 32], P(None, 'head'), may hold values from -0.125 to 0.125
- write_weight: bfloat16 [2048, 32], P(None, 'head'), may hold values from -0.125 to 0.125
- decay_bias: float32 [32], P('head'), may hold values from -2 to 2
- decay_log: float32 [32], P('head'), may hold values from -11 to -2
- write_bias: float32 [32], P('head'), may hold values from -9 to 0
- start_state: float32 [16, 32, 128, 128], P('seq', 'head'), may hold values from -4 to 4
Outputs:
- grad_queries: bfloat16 [2048, 32, 128], P('seq', 'head')
- grad_keys: bfloat16 [2048, 32, 128], P('seq', 'head')
- grad_values: bfloat16 [2048, 32, 128], P('seq', 'head')
- grad_hidden: bfloat16 [2048, 2048], P('seq', 'head')
- grad_decay_weight: float32 [2048, 32], P(None, 'head')
- grad_write_weight: float32 [2048, 32], P(None, 'head')
All inputs are finite; a program needn't handle non-finite values.
Results may differ from a plain program's by a relative error of at most 0.014.
Values may be sent and summed in bfloat16 or wider, within the bound.
A program may use at most 128 MiB of HBM per device.

v0:
```python
from functools import partial

import jax
import jax.numpy as jnp
from jax import lax
from jax.experimental import pallas as pl
from jax.experimental.pallas import tpu as pltpu
from jax.sharding import PartitionSpec as P

EPSILON = 1e-06
HI = lax.Precision.HIGHEST
F32 = jnp.float32
BF = jnp.bfloat16


def mm(a, b, ca=1, cb=0):
    return lax.dot_general(
        a.astype(BF), b.astype(BF), (((ca,), (cb,)), ((), ())), preferred_element_type=F32
    )


def unit(x):
    r = lax.rsqrt(jnp.sum(x * x, axis=1, keepdims=True) + EPSILON)
    return x * r, r


def unit_back(d, n, r):
    return r * (d - n * jnp.sum(n * d, axis=1, keepdims=True))


def indices(c):
    row = lax.broadcasted_iota(jnp.int32, (c, c), 0)
    col = lax.broadcasted_iota(jnp.int32, (c, c), 1)
    return row, col


def local_first(q, k, v, s0, rows):
    c = q.shape[0]
    row, col = indices(c)
    cols = rows.T
    g_col, beta = cols[:, 0:1], cols[:, 1:2]
    g_row = rows[0:1, :]
    g_last = g_row[:, c - 1 : c]
    cd = jnp.exp(g_col)
    to_end = jnp.exp(g_last - g_col)
    lower = row >= col
    gamma = jnp.where(lower, jnp.exp(jnp.where(lower, g_col - g_row, 0.0)), 0.0)
    gamma_strict = jnp.where(row > col, gamma, 0.0)
    qn, rq = unit(q.astype(F32))
    kn, _ = unit(k.astype(F32))
    qb, kb, sb = qn.astype(BF), kn.astype(BF), s0.astype(BF)
    gram = gamma_strict * mm(kb, kb, 1, 1)
    p = gamma * mm(qb, kb, 1, 1)
    z = v.astype(F32) - cd * mm(kb, sb)
    a = beta * gram
    return qn, rq, qb, kn, kb, sb, p, z, a, gram, gamma, gamma_strict, beta, cd, to_end


def inverses(couplings):
    c = couplings[0].shape[0]
    row, col = indices(c)
    invs = [
        jnp.where(row == col, 1.0, jnp.where((row ^ col) == 1, -a, 0.0)) for a in couplings
    ]
    level = 1
    while (2 << level) <= c:
        near = ((row >> level) ^ (col >> level)) == 1
        halves = [mm(x, jnp.where(near, a, 0.0)) for x, a in zip(invs, couplings)]
        invs = [x - mm(y, x) for x, y in zip(invs, halves)]
        level += 1
    return invs


def local_rest(do, inv, first):
    qn, rq, qb, kn, kb, sb, p, z, a, gram, gamma, gamma_strict, beta, cd, to_end = first
    ib = inv.astype(BF)
    ub = mm(ib, beta * z).astype(BF)
    ptdo = mm(p, do, 0, 0)
    w0 = mm(ib, ptdo, 0, 0)
    nb = mm(ib, to_end * kn, 0, 0).astype(BF)
    bck = ((beta * cd) * kn).astype(BF)
    off = mm(cd * qn, do, 0, 0) - mm(bck, w0, 0, 0)
    tt = mm(bck, nb, 0, 0)
    dp = mm(do, ub, 1, 1)
    dos = cd * mm(do, sb, 1, 1)
    gdp = (gamma * dp).astype(BF)
    dq = unit_back(dos + mm(gdp, kb), qn, rq)
    dk0 = mm(gdp, qb, 0, 0)
    t = dp * p
    dg0 = jnp.sum((t + dos * qn).T, axis=0, keepdims=True) - jnp.sum(t, axis=0, keepdims=True)
    return dq, ub, w0, nb, tt, off, z, gram, gamma_strict, dk0, dg0


def carry_head(k, v, s0, e, rows, ub, w0, nb, z, gram, gamma_strict, dk0, dg0):
    c = k.shape[0]
    row, col = indices(c)
    cols = rows.T
    g_col, beta = cols[:, 0:1], cols[:, 1:2]
    g_last = rows[0:1, c - 1 : c]
    cd = jnp.exp(g_col)
    to_end = jnp.exp(g_last - g_col)
    kn, rk = unit(k.astype(F32))
    kb = kn.astype(BF)
    w = w0 + mm(nb, e)
    wb = w.astype(BF)
    dv = beta * w
    da = -mm(wb, ub, 1, 1)
    ws = mm(wb, s0, 1, 1)
    ue = to_end * mm(ub, e, 1, 1)
    dkk = (beta * gamma_strict * da).astype(BF)
    dkn = dk0 - (beta * cd) * ws + mm(dkk, kb) + mm(dkk, kb, 0, 0) + ue
    dk = unit_back(dkn, kn, rk)
    dagram = da * gram
    t = beta * dagram
    s = kn * ue
    dbeta = jnp.sum((dagram + w * z).T, axis=0, keepdims=True)
    dg = dg0 - jnp.sum(t, axis=0, keepdims=True)
    dg = dg + jnp.sum((t - dv * (v.astype(F32) - z) - s).T, axis=0, keepdims=True)
    tail = jnp.sum(s, keepdims=True) + jnp.exp(g_last) * jnp.sum(s0 * e.astype(F32), keepdims=True)
    lane = lax.broadcasted_iota(jnp.int32, (1, c), 1)
    dg = dg + jnp.where(lane == c - 1, tail, 0.0)
    return dv, dk, dg, dbeta


def local_kernel(q, k, v, do, s0, rows, dq, ub, w0, nb, tt, off, z, gram, gs, dk0, dg0):
    firsts = [local_first(q[i], k[i], v[i], s0[i], rows[i]) for i in range(q.shape[0])]
    invs = inverses([first[8] for first in firsts])
    for i in range(q.shape[0]):
        outs = local_rest(do[i], invs[i], firsts[i])
        for ref, value in zip((dq, ub, w0, nb, tt, off, z, gram, gs, dk0, dg0), outs):
            ref[i] = value.astype(ref.dtype)


def carry_kernel(k, v, s0, e, rows, ub, w0, nb, z, gram, gs, dk0, dg0, dv, dk, dg, dbeta):
    for i in range(k.shape[0]):
        outs = carry_head(
            k[i], v[i], s0[i], e[i], rows[i], ub[i], w0[i], nb[i], z[i], gram[i], gs[i], dk0[i], dg0[i]
        )
        for ref, value in zip((dv, dk, dg, dbeta), outs):
            ref[i] = value.astype(ref.dtype)


def chain_kernel(n, tt, off, rows, e_out, inbuf, outbuf, send_sem, recv_sem):
    me = lax.axis_index("seq")
    heads, c = tt.shape[0], rows.shape[2]
    barrier = pltpu.get_barrier_semaphore()
    mesh_id = pl.DeviceIdType.MESH

    @pl.when(me > 0)
    def _():
        pl.semaphore_signal(barrier, inc=1, device_id={"seq": me - 1}, device_id_type=mesh_id)

    @pl.when(me < n - 1)
    def _():
        pl.semaphore_signal(barrier, inc=1, device_id={"seq": me + 1}, device_id_type=mesh_id)

    peers = jnp.where(me > 0, 1, 0) + jnp.where(me < n - 1, 1, 0)
    pl.semaphore_wait(barrier, peers)

    def copy(h):
        return pltpu.make_async_remote_copy(
            src_ref=outbuf.at[h],
            dst_ref=inbuf.at[h],
            send_sem=send_sem.at[h],
            recv_sem=recv_sem.at[h],
            device_id={"seq": me - 1},
            device_id_type=mesh_id,
        )

    @pl.when(me == n - 1)
    def _():
        def first(h, _):
            outbuf[h] = off[h].astype(BF)
            copy(h).start()
            e_out[h] = jnp.zeros(e_out.shape[1:], e_out.dtype)
            return 0

        lax.fori_loop(0, heads, first, 0)

    @pl.when(me < n - 1)
    def _():
        def step(h, _):
            copy(h).wait_recv()
            e = inbuf[h]

            @pl.when(me > 0)
            def _():
                cdl = jnp.exp(rows[h, 0:1, c - 1 : c])
                outbuf[h] = (off[h] + cdl * e.astype(F32) - mm(tt[h], e)).astype(BF)
                copy(h).start()

            e_out[h] = e
            return 0

        lax.fori_loop(0, heads, step, 0)

    @pl.when(me > 0)
    def _():
        def done(h, _):
            copy(h).wait_send()
            return 0

        lax.fori_loop(0, heads, done, 0)


def sums_kernel(n, m, terms, halves, total, mine, got, part, gathered, got_half, sems, half_sems):
    me, side = lax.axis_index("seq"), lax.axis_index("head")
    mesh_id = pl.DeviceIdType.MESH
    barrier = pltpu.get_barrier_semaphore()

    def greet(d, _):
        pl.semaphore_signal(
            barrier, inc=1, device_id={"seq": lax.rem(me + d, n)}, device_id_type=mesh_id
        )
        return 0

    def greet_side(d, _):
        pl.semaphore_signal(
            barrier, inc=1, device_id={"head": lax.rem(side + d, m)}, device_id_type=mesh_id
        )
        return 0

    lax.fori_loop(1, n, greet, 0)
    lax.fori_loop(1, m, greet_side, 0)
    pl.semaphore_wait(barrier, n + m - 2)

    def scatter(to, source):
        return pltpu.make_async_remote_copy(
            src_ref=terms.at[to], dst_ref=got.at[source],
            send_sem=sems.at[0, to], recv_sem=sems.at[1, source],
            device_id={"seq": to}, device_id_type=mesh_id,
        )

    def gather(to, source):
        return pltpu.make_async_remote_copy(
            src_ref=part, dst_ref=gathered.at[source],
            send_sem=sems.at[2, to], recv_sem=sems.at[3, source],
            device_id={"seq": to}, device_id_type=mesh_id,
        )

    def swap(to, source):
        return pltpu.make_async_remote_copy(
            src_ref=halves.at[to], dst_ref=got_half.at[source],
            send_sem=half_sems.at[0, to], recv_sem=half_sems.at[1, source],
            device_id={"head": to}, device_id_type=mesh_id,
        )

    def ahead(d):
        return lax.rem(me + d, n)

    def behind(d):
        return lax.rem(me + n - d, n)

    def side_ahead(d):
        return lax.rem(side + d, m)

    def side_behind(d):
        return lax.rem(side + m - d, m)

    def run(count, body):
        def step(d, _):
            body(d)
            return 0

        lax.fori_loop(1, count, step, 0)

    run(n, lambda d: scatter(ahead(d), me).start())
    run(m, lambda d: swap(side_ahead(d), side).start())

    def add(d, acc):
        source = behind(d)
        scatter(source, source).wait_recv()
        return acc + got[source]

    acc = lax.fori_loop(1, n, add, terms[me])
    part[...] = acc
    total[me] = acc
    run(n, lambda d: gather(ahead(d), me).start())

    def add_half(d, acc):
        source = side_behind(d)
        swap(source, source).wait_recv()
        return acc + got_half[source].astype(F32)

    mine[...] = lax.fori_loop(1, m, add_half, halves[side].astype(F32)).astype(BF)

    def place(d):
        source = behind(d)
        gather(source, source).wait_recv()
        total[source] = gathered[source]

    run(n, place)
    run(n, lambda d: scatter(ahead(d), me).wait_send())
    run(n, lambda d: gather(ahead(d), me).wait_send())
    run(m, lambda d: swap(side_ahead(d), side).wait_send())


def sums_part(n, m, terms, halves):
    vm = pl.BlockSpec(memory_space=pltpu.VMEM)
    return pl.pallas_call(
        partial(sums_kernel, n, m),
        out_shape=(
            jax.ShapeDtypeStruct(terms.shape, F32),
            jax.ShapeDtypeStruct(halves.shape[1:], BF),
        ),
        in_specs=[vm] * 2,
        out_specs=(vm, vm),
        scratch_shapes=[
            pltpu.VMEM(terms.shape, F32),
            pltpu.VMEM(terms.shape[1:], F32),
            pltpu.VMEM(terms.shape, F32),
            pltpu.VMEM(halves.shape, BF),
            pltpu.SemaphoreType.DMA((4, n)),
            pltpu.SemaphoreType.DMA((2, m)),
        ],
        compiler_params=pltpu.CompilerParams(collective_id=1, has_side_effects=True),
    )(terms, halves)


def per_head(kernel, group, ins, outs):
    heads = ins[0].shape[0]

    def spec(a):
        return pl.BlockSpec((group,) + a.shape[1:], lambda h: (h, 0, 0))

    return pl.pallas_call(
        kernel,
        grid=(heads // group,),
        out_shape=outs,
        in_specs=[spec(a) for a in ins],
        out_specs=[spec(a) for a in outs],
        compiler_params=pltpu.CompilerParams(vmem_limit_bytes=48 * 1024 * 1024),
    )(*ins)


def local_part(q, k, v, do, s0, rows):
    h, c, dk = q.shape
    dv = v.shape[2]
    sd = jax.ShapeDtypeStruct
    outs = [
        sd((h, c, dk), BF), sd((h, c, dv), BF), sd((h, c, dv), F32), sd((h, c, dk), BF),
        sd((h, dk, dk), BF), sd((h, dk, dv), F32), sd((h, c, dv), F32), sd((h, c, c), F32),
        sd((h, c, c), F32), sd((h, c, dk), F32), sd((h, 1, c), F32),
    ]
    return per_head(local_kernel, min(8, h), (q, k, v, do, s0, rows), outs)


def carry_part(k, v, s0, e, rows, saved):
    h, c, dk = k.shape
    dv = v.shape[2]
    sd = jax.ShapeDtypeStruct
    outs = [sd((h, c, dv), BF), sd((h, c, dk), BF), sd((h, 1, c), F32), sd((h, 1, c), F32)]
    return per_head(carry_kernel, 4, (k, v, s0, e, rows) + saved, outs)


def chain_part(n, tt, off, rows):
    vm = pl.BlockSpec(memory_space=pltpu.VMEM)
    h = tt.shape[0]
    return pl.pallas_call(
        partial(chain_kernel, n),
        out_shape=jax.ShapeDtypeStruct(off.shape, BF),
        in_specs=[vm] * 3,
        out_specs=vm,
        scratch_shapes=[
            pltpu.VMEM(off.shape, BF),
            pltpu.VMEM(off.shape, BF),
            pltpu.SemaphoreType.DMA((h,)),
            pltpu.SemaphoreType.DMA((h,)),
        ],
        compiler_params=pltpu.CompilerParams(collective_id=0, has_side_effects=True),
    )(tt, off, rows)


def gates(hidden_in, both, decay_bias, decay_log, write_bias):
    h = decay_bias.shape[0]
    logits = lax.dot_general(
        both, hidden_in, (((0,), (1,)), ((), ())), preferred_element_type=F32
    )
    pre = logits[:h] + decay_bias[:, None]
    rate = jnp.exp(decay_log)[:, None]
    beta = jax.nn.sigmoid(logits[h:] + write_bias[:, None])
    log_decay = -rate * jax.nn.softplus(pre)
    c = log_decay.shape[1]
    ones = jnp.triu(jnp.ones((c, c), F32))
    g = jnp.dot(log_decay, ones, precision=HI)
    return pre, rate, beta, g, ones


def shards(
    queries,
    key_vectors,
    values,
    out_grad,
    hidden_in,
    decay_weight,
    write_weight,
    decay_bias,
    decay_log,
    write_bias,
    start_state,
):
    n = lax.axis_size("seq")
    both = jnp.concatenate([decay_weight, write_weight], axis=1)
    pre, rate, beta, g, ones = gates(hidden_in, both, decay_bias, decay_log, write_bias)
    h, c = g.shape
    rows = jnp.concatenate(
        [g[:, None], beta[:, None], jnp.zeros((h, 6, c), F32)], axis=1
    )
    q, k, v, do = (jnp.swapaxes(a, 0, 1) for a in (queries, key_vectors, values, out_grad))
    s0 = start_state[0]
    dq, ub, w0, nb, tt, off, z, gram, gs, dk0, dg0 = local_part(q, k, v, do, s0, rows)
    e = chain_part(n, tt, off, rows)
    dv, dk, dg, dbeta = carry_part(k, v, s0, e, rows, (ub, w0, nb, z, gram, gs, dk0, dg0))
    dlog = jnp.dot(dg[:, 0], ones.T, precision=HI)
    decay_grads = (-dlog * rate * jax.nn.sigmoid(pre)).astype(BF)
    write_grads = (dbeta[:, 0] * beta * (1.0 - beta)).astype(BF)
    grads = jnp.concatenate([decay_grads, write_grads], axis=0)
    weight_terms = jnp.dot(grads, hidden_in, preferred_element_type=F32)
    width = hidden_in.shape[1]
    terms = jnp.swapaxes(weight_terms.reshape(2 * h, n, width // n), 0, 1)
    m = lax.axis_size("head")
    halves = lax.dot_general(
        jnp.broadcast_to(grads, (m,) + grads.shape),
        both.reshape(m, width // m, 2 * h),
        (((1,), (2,)), ((0,), (0,))),
        preferred_element_type=F32,
    ).astype(BF)
    total, grad_hidden = sums_part(n, m, terms, halves)
    total = jnp.swapaxes(total, 0, 1).reshape(2 * h, width)
    return (
        jnp.swapaxes(dq, 0, 1),
        jnp.swapaxes(dk, 0, 1),
        jnp.swapaxes(dv, 0, 1),
        grad_hidden,
        total[:h].T,
        total[h:].T,
    )


def solution(mesh):
    placed = (
        P("seq", "head", None),
        P("seq", "head", None),
        P("seq", "head", None),
        P("seq", "head", None),
        P("seq", None),
        P(None, "head"),
        P(None, "head"),
        P("head"),
        P("head"),
        P("head"),
        P("seq", "head", None, None),
    )
    return jax.shard_map(
        shards,
        mesh=mesh,
        in_specs=placed,
        out_specs=(
            P("seq", "head", None),
            P("seq", "head", None),
            P("seq", "head", None),
            P("seq", "head"),
            P(None, "head"),
            P(None, "head"),
        ),
        check_vma=False,
    )
```

profile of v0, /device:TPU:0, one launch (start us, length us, event | category | flops | bytes accessed | tf_op | source)
XLA Modules:
  0.0 130.9 jit_solution(1552650384822115778)
XLA Ops:
  0.6 0.0 copy-start
  0.7 0.0 copy-start.17
  0.7 0.1 pad.4.clone
  0.8 0.6 copy-done.17
  1.4 0.0 copy-start.16
  1.4 0.9 constant_dynamic-update-slice_fusion.1
  2.3 0.0 copy-done.15
  2.3 0.0 copy-start.11
  2.3 0.0 copy-done
  2.3 0.3 fusion.35
  2.6 0.0 copy-done.18
  2.6 0.2 fusion.6
  2.8 0.0 copy-done.16
  2.8 0.1 fusion.19
  2.9 0.1 maximum_maximum_fusion.rows
  3.0 0.3 copy-done.10
  3.3 0.2 copy-done.11
  3.5 0.3 copy_bitcast_fusion.2
  3.8 0.8 copy-done.12
  4.6 0.2 copy-done.13
  4.7 0.3 copy_bitcast_fusion
  5.0 0.0 copy-done.3
  5.0 15.6 %shard_map.154 = (bf16[16,128,128]{2,1,0:T(8,128)(2,1)S(1)}, bf16[16,128,128]{2,1,0:T(8,128)(2,1)S(1)}, f32[16,128,128]{2,1,0:T(8,128)S(1)}, bf16[16,128,128]{2,...) custom-call(bf16[16,128,128]{2,1,0:T(8,128)(2,1)S(1)} %get-tuple-ele, ...), custom_call_target="tpu_custom_call" | custom-call | tf_op jit(solution)/shard_map/pallas_call | solution.py:326
  20.6 1.0 copy-done.5
  21.6 0.8 copy-done.7
  22.4 0.8 copy-done.9
  23.2 1.1 copy.32
  24.3 67.0 %shard_map.155.e = bf16[16,128,128]{2,1,0:T(8,128)(2,1)} custom-call(bf16[16,128,128]{2,1,0:T(8,128)(2,1)} %copy-done.9, f32[16,128,128]{2,1,0:T(8,128)} %get-tuple-element.25.off, f32[16,8,128]{2,1,0:T(8,128)} %copy-done.3), custom_call_target="tpu_custom_call" | custom-call | tf_op jit(solution)/shard_map/pallas_call | solution.py:359
  91.3 0.0 copy-done.1
  91.3 0.0 copy-done.4
  91.4 0.0 copy-start.2
  91.4 1.0 copy-done.2
  92.4 1.2 copy-done.6
  93.6 1.0 copy-done.8
  94.7 9.5 %shard_map.156 = (bf16[16,128,128]{2,1,0:T(8,128)(2,1)S(1)}, bf16[16,128,128]{2,1,0:T(8,128)(2,1)S(1)}, f32[16,1,128]{2,1,0:T(1,128)S(1)}, f32[16,1,128]{2,1,0:T(1,128)S(1)}) custom-call(bf16[16,128,128]{2,1,0:T(8,128)(2,1)S(1)} %get-tuple-element.58.k, bf16[16,128,128]{2,1,0:T(8,128)(2,1)S(1)} %get-tuple-element.57.v, f32[16,128,128]{2,1,0:T(8,128)S(1)} %bitcast.50, ...), custom_call_target="tpu_custom_call" | custom-call | tf_op jit(solution)/shard_map/pallas_call | solution.py:326
  104.2 1.1 copy.33
  105.4 1.1 copy.34
  106.5 0.3 fusion.2
  106.8 0.1 multiply_convert_fusion
  106.9 0.2 convolution_bitcast_fusion
  107.1 0.7 copy.50
  107.8 1.1 convolution_convert_fusion.halves
  109.0 18.8 %shard_map.157 = (f32[16,32,128]{2,1,0:T(8,128)}, bf16[128,1024]{1,0:T(8,128)(2,1)}) custom-call(f32[16,32,128]{2,1,0:T(8,128)} %bitcast.56, bf16[2,128,1024]{2,1,0:T(8,128)(2,1)} %convolution_convert_fusion.halves), custom_call_target="tpu_custom_call" | custom-call | tf_op jit(solution)/shard_map/pallas_call | solution.py:300
  127.8 1.0 slice_bitcast_fusion
  128.8 0.0 copy-start.14
  128.8 0.7 copy.51
  129.5 0.7 copy.52
  130.2 0.7 copy.55
  (19 shorter events, 0.0 us)
Async XLA Ops:
  0.6 1.7 %copy-start = (bf16[128,2048]{1,0:T(8,128)(2,1)S(1)}, bf16[128,2048]{1,0:T(8,128)(2,1)}, u32[]{:S(2)}) copy-start(bf16[128,2048]{1,0:T(8,128)(2,1)} %param.15) | copy-start | bytes 1572868
  0.7 0.7 copy-start.17
  1.4 0.9 copy-start.15
  1.4 1.2 copy-start.18
  1.4 1.5 %copy-start.16 = (f32[16]{0:T(128)S(1)}, f32[16]{0:T(128)}, u32[]{:S(2)}) copy-start(f32[16]{0:T(128)} %param.20) | copy-start | bytes 196
  2.3 1.0 copy-start.10
  2.3 1.2 copy-start.11
  3.5 1.5 %copy-start.3 = (f32[16,8,128]{2,1,0:T(8,128)}, f32[16,8,128]{2,1,0:T(8,128)S(1)}, u32[]{:S(2)}) copy-start(f32[16,8,128]{2,1,0:T(8,128)S(1)} %maximum_maximum_fusion.rows) | copy-start | bytes 196612
  3.5 1.1 copy-start.12
  3.5 1.2 copy-start.13
  20.6 1.0 copy-start.5
  21.6 0.8 copy-start.7
  22.4 0.8 copy-start.9
  24.3 67.0 %copy-start.1 = (f32[1,16,128,128]{3,2,1,0:T(8,128)S(1)}, f32[1,16,128,128]{3,2,1,0:T(8,128)}, u32[]{:S(2)}) copy-start(f32[1,16,128,128]{3,2,1,0:T(8,128)} %param.21) | copy-start | bytes 3145732
  24.3 67.0 %copy-start.4 = (f32[16,8,128]{2,1,0:T(8,128)S(1)}, f32[16,8,128]{2,1,0:T(8,128)}, u32[]{:S(2)}) copy-start(f32[16,8,128]{2,1,0:T(8,128)} %copy-done.3) | copy-start | bytes 196612
  91.4 1.0 copy-start.2
  92.4 1.2 copy-start.6
  93.6 1.0 copy-start.8
  128.8 1.3 %copy-start.14 = (bf16[128,1024]{1,0:T(8,128)(2,1)S(1)}, bf16[128,1024]{1,0:T(8,128)(2,1)}, u32[]{:S(2)}) copy-start(bf16[128,1024]{1,0:T(8,128)(2,1)} %get-tuple-element.69) | copy-start | bytes 786436
where the time goes:
time: 131 us
  Pallas kernels  111 us (85%)
  local copies, waits for them, and re-layouts  16.6 us (13%)
  matrix products  2.13 us (2%)
    pallas_call x1, Pallas kernels, chain_part(): pl.pallas_call(partial(chain_kernel, n), out_shape=jax.ShapeDtypeStruct(o...  67 us
    pallas_call x2, Pallas kernels, per_head(): pl.pallas_call(kernel, grid=(heads // group,), out_shape=outs, in_specs=[...  25.2 us
    pallas_call x1, Pallas kernels, sums_part(): pl.pallas_call(partial(sums_kernel, n, m), out_shape=(jax.ShapeDtypeStruc...  18.8 us
    unnamed x44, local copies, waits for them, and re-layouts  13.9 us

commit v1 on v0

v1 whole, which is shorter than its diff:
```python
from functools import partial

import jax
import jax.numpy as jnp
from jax import lax
from jax.experimental import pallas as pl
from jax.experimental.pallas import tpu as pltpu
from jax.sharding import PartitionSpec as P

EPSILON = 1e-06
HI = lax.Precision.HIGHEST
F32 = jnp.float32
BF = jnp.bfloat16


def mm(a, b, ca=1, cb=0):
    return lax.dot_general(
        a.astype(BF), b.astype(BF), (((ca,), (cb,)), ((), ())), preferred_element_type=F32
    )


def unit(x):
    r = lax.rsqrt(jnp.sum(x * x, axis=1, keepdims=True) + EPSILON)
    return x * r, r


def unit_back(d, n, r):
    return r * (d - n * jnp.sum(n * d, axis=1, keepdims=True))


def indices(c):
    row = lax.broadcasted_iota(jnp.int32, (c, c), 0)
    col = lax.broadcasted_iota(jnp.int32, (c, c), 1)
    return row, col


def inverses(couplings):
    c = couplings[0].shape[0]
    row, col = indices(c)
    invs = [
        jnp.where(row == col, 1.0, jnp.where((row ^ col) == 1, -a, 0.0)) for a in couplings
    ]
    level = 1
    while (2 << level) <= c:
        near = ((row >> level) ^ (col >> level)) == 1
        halves = [mm(x, jnp.where(near, a, 0.0)) for x, a in zip(invs, couplings)]
        invs = [x - mm(y, x) for x, y in zip(invs, halves)]
        level += 1
    return invs


def decays(rows):
    c = rows.shape[1]
    cols = rows.T
    g_col, beta = cols[:, 0:1], cols[:, 1:2]
    g_row = rows[0:1, :]
    g_last = g_row[:, c - 1 : c]
    return g_col, g_row, g_last, beta, jnp.exp(g_col), jnp.exp(g_last - g_col)


def local_first(q, k, rows):
    c = q.shape[0]
    row, col = indices(c)
    g_col, g_row, g_last, beta, cd, to_end = decays(rows)
    lower = row >= col
    gamma = jnp.where(lower, jnp.exp(jnp.where(lower, g_col - g_row, 0.0)), 0.0)
    gs = jnp.where(row > col, gamma, 0.0)
    qn, _ = unit(q.astype(F32))
    kn, _ = unit(k.astype(F32))
    kb = kn.astype(BF)
    grams = mm(jnp.concatenate([qn.astype(BF), kb], axis=0), kb, 1, 1)
    p = gamma * grams[:c]
    gram = gs * grams[c:]
    return qn, kn, p, gram, gs, beta * gram, beta, cd, to_end, jnp.exp(g_last)


def local_map(do, inv, first):
    qn, kn, p, gram, gs, a, beta, cd, to_end, last = first
    c = qn.shape[0]
    ib = inv.astype(BF)
    ptdo = mm(p, do, 0, 0)
    both = mm(ib, jnp.concatenate([ptdo.astype(BF), (to_end * kn).astype(BF)], axis=1), 0, 0)
    dv = do.shape[1]
    bck = ((beta * cd) * kn).astype(BF)
    prod = mm(bck, both, 0, 0)
    off = mm(cd * qn, do, 0, 0) - prod[:, :dv]
    return ib, both[:, :dv], both[:, dv:].astype(BF), off, prod[:, dv:]


def local_rest(q, k, v, do, s0, rows, ib, p, gs):
    c = q.shape[0]
    row, col = indices(c)
    g_col, g_row, g_last, beta, cd, to_end = decays(rows)
    qn, rq = unit(q.astype(F32))
    kn, _ = unit(k.astype(F32))
    qb, kb, sb = qn.astype(BF), kn.astype(BF), s0.astype(BF)
    gamma = jnp.where(row == col, 1.0, gs)
    z = v.astype(F32) - cd * mm(kb, sb)
    ub = mm(ib, beta * z).astype(BF)
    prod = mm(do, jnp.concatenate([ub, sb], axis=0), 1, 1)
    dp, dos = prod[:, :c], cd * prod[:, c:]
    gdp = (gamma * dp).astype(BF)
    dq = unit_back(dos + mm(gdp, kb), qn, rq)
    dk0 = mm(gdp, qb, 0, 0)
    t = dp * p
    dg0 = jnp.sum((t + dos * qn).T, axis=0, keepdims=True) - jnp.sum(t, axis=0, keepdims=True)
    return dq, z, ub, dk0, dg0


def carry_head(k, v, s0, e, rows, ub, w0, nb, z, gram, gs, dk0, dg0):
    c = k.shape[0]
    g_col, g_row, g_last, beta, cd, to_end = decays(rows)
    kn, rk = unit(k.astype(F32))
    kb = kn.astype(BF)
    w = w0 + mm(nb, e)
    wb = w.astype(BF)
    dv = beta * w
    prod = mm(wb, jnp.concatenate([ub, s0.astype(BF)], axis=0), 1, 1)
    da, ws = -prod[:, :c], prod[:, c:]
    ue = to_end * mm(ub, e, 1, 1)
    dkk = (beta * gs * da).astype(BF)
    dkn = dk0 - (beta * cd) * ws + mm(dkk, kb) + mm(dkk, kb, 0, 0) + ue
    dk = unit_back(dkn, kn, rk)
    dagram = da * gram
    t = beta * dagram
    s = kn * ue
    dbeta = jnp.sum((dagram + w * z).T, axis=0, keepdims=True)
    dg = dg0 - jnp.sum(t, axis=0, keepdims=True)
    dg = dg + jnp.sum((t - dv * (v.astype(F32) - z) - s).T, axis=0, keepdims=True)
    tail = jnp.sum(s, keepdims=True) + jnp.exp(g_last) * jnp.sum(s0 * e.astype(F32), keepdims=True)
    lane = lax.broadcasted_iota(jnp.int32, (1, c), 1)
    dg = dg + jnp.where(lane == c - 1, tail, 0.0)
    return dv, dk, dg, dbeta


def split3(x):
    hi = x.astype(BF)
    rest = x - hi.astype(F32)
    mid = rest.astype(BF)
    return hi, mid, (rest - mid.astype(F32)).astype(BF)


def group_size(n, heads):
    size = 1
    while (2 * size) ** 2 <= n and heads % (2 * size) == 0 and n % (2 * size) == 0:
        size *= 2
    return size


def whole_kernel(
    n, m, size,
    q, k, v, do, s0, rows, fac, hidden, weights,
    dq, dk, dv, gh, gd, gw,
    pmat, gram, gs, invs, w0, nb, z, ub, dk0, dg0, dgs, dbs,
    maps, maps_in, tcomp, bcomp, gcomp, zin, zout, eout, ein,
    tbuf, got, part, gathered, ggot, wgot,
    map_sems, map_recv, z_sems, e_send, e_recv, sum_sems, head_sems,
):
    me, side = lax.axis_index("seq"), lax.axis_index("head")
    mesh_id = pl.DeviceIdType.MESH
    heads, c, dkk = q.shape
    dvv = v.shape[2]
    own = heads // size
    planes = n // size
    plane, rank = me // size, lax.rem(me, size)
    lag = planes - 1 - plane
    barrier = pltpu.get_barrier_semaphore()

    def run(low, high, body):
        def step(d, _):
            body(d)
            return 0

        lax.fori_loop(low, high, step, 0)

    def ahead(d):
        return lax.rem(me + d, n)

    def behind(d):
        return lax.rem(me + n - d, n)

    def side_ahead(d):
        return lax.rem(side + d, m)

    def side_behind(d):
        return lax.rem(side + m - d, m)

    def greet(d):
        pl.semaphore_signal(barrier, inc=1, device_id={"seq": ahead(d)}, device_id_type=mesh_id)

    def greet_side(d):
        pl.semaphore_signal(
            barrier, inc=1, device_id={"head": side_ahead(d)}, device_id_type=mesh_id
        )

    run(1, n, greet)
    run(1, m, greet_side)

    def send_map(b, to, source):
        return pltpu.make_async_remote_copy(
            src_ref=maps.at[b, to], dst_ref=maps_in.at[b, source],
            send_sem=map_sems.at[b, to], recv_sem=map_recv.at[b, source],
            device_id={"seq": plane * size + to}, device_id_type=mesh_id,
        )

    def send_plane(b):
        return pltpu.make_async_remote_copy(
            src_ref=zout.at[b], dst_ref=zin.at[b],
            send_sem=z_sems.at[0, b], recv_sem=z_sems.at[1, b],
            device_id={"seq": lax.rem(me + n - size, n)}, device_id_type=mesh_id,
        )

    def send_back(b, to, owner):
        return pltpu.make_async_remote_copy(
            src_ref=eout.at[b, to], dst_ref=ein.at[owner * own + b],
            send_sem=e_send.at[b, to], recv_sem=e_recv.at[owner * own + b],
            device_id={"seq": plane * size + to}, device_id_type=mesh_id,
        )

    def scatter(to, source):
        return pltpu.make_async_remote_copy(
            src_ref=tbuf.at[to], dst_ref=got.at[source],
            send_sem=sum_sems.at[0, to], recv_sem=sum_sems.at[1, source],
            device_id={"seq": to}, device_id_type=mesh_id,
        )

    def gather(to, source):
        return pltpu.make_async_remote_copy(
            src_ref=part, dst_ref=gathered.at[source],
            send_sem=sum_sems.at[2, to], recv_sem=sum_sems.at[3, source],
            device_id={"seq": to}, device_id_type=mesh_id,
        )

    def send_weights(to, source):
        return pltpu.make_async_remote_copy(
            src_ref=weights.at[to], dst_ref=wgot.at[source],
            send_sem=head_sems.at[0, to], recv_sem=head_sems.at[1, source],
            device_id={"head": to}, device_id_type=mesh_id,
        )

    def send_grads(to, source):
        return pltpu.make_async_remote_copy(
            src_ref=ggot.at[side], dst_ref=ggot.at[source],
            send_sem=head_sems.at[2, to], recv_sem=head_sems.at[3, source],
            device_id={"head": to}, device_id_type=mesh_id,
        )

    @pl.when(lag == 0)
    def _():
        zin[...] = jnp.zeros(zin.shape, BF)

    def local_batch(b):
        hs = [j * own + b for j in range(size)]
        firsts = [local_first(q[h], k[h], rows[h]) for h in hs]
        solved = inverses([first[5] for first in firsts])
        for j, h in enumerate(hs):
            first = firsts[j]
            ib, w0_, nb_, off, tt = local_map(do[h], solved[j], first)
            pmat[h], gram[h], gs[h] = first[2], first[3], first[4]
            invs[h], w0[h], nb[h] = ib, w0_, nb_
            last = jnp.broadcast_to(first[9], (8, dvv))
            high = last.astype(BF)
            low = (last - high.astype(F32)).astype(BF)
            message = jnp.concatenate([tt.astype(BF), off.astype(BF), high, low], axis=0)
            maps[b, j] = message

            @pl.when(rank == j)
            def _():
                maps_in[b, j] = message

    def local_sends(b):
        for j in range(size):

            @pl.when(rank != j)
            def _():
                send_map(b, j, rank).start()

    def piece(b, p):
        t = maps_in[b, p, :dkk]
        off = maps_in[b, p, dkk : 2 * dkk].astype(F32)
        ends = maps_in[b, p, 2 * dkk :].astype(F32)
        return t, off, ends[0:1] + ends[8:9]

    def compose(b):
        for p in range(size):

            @pl.when(rank != p)
            def _():
                send_map(b, p, p).wait_recv()

        t, bc, g = piece(b, size - 1)
        tc = t.astype(F32)
        for p in range(size - 2, -1, -1):
            t, off, last = piece(b, p)
            prod = mm(t, jnp.concatenate([tc.astype(BF), bc.astype(BF)], axis=1))
            tc = last * tc + g * t.astype(F32) - prod[:, :dkk]
            bc = last * bc + off - prod[:, dkk:]
            g = last * g
        tcomp[b] = tc.astype(BF)
        bcomp[b] = bc
        gcomp[b] = jnp.broadcast_to(g, gcomp.shape[1:])

    def hand_on(b):
        @pl.when(lag > 0)
        def _():
            send_plane(b).wait_recv()

        eb = zin[b]

        @pl.when(plane > 0)
        def _():
            e = gcomp[b, 0:1] * eb.astype(F32) + bcomp[b] - mm(tcomp[b], eb)
            zout[b] = e.astype(BF)
            send_plane(b).start()

        e = eb.astype(F32)
        for p in range(size - 1, -1, -1):
            eout[b, p] = eb

            @pl.when(rank == p)
            def _():
                ein[rank * own + b] = eb

            @pl.when(rank != p)
            def _():
                send_back(b, p, rank).start()

            if p > 0:
                t, off, last = piece(b, p)
                e = last * e + off - mm(t, eb)
                eb = e.astype(BF)

    def rest_batch(b):
        for j in range(size):
            h = j * own + b
            outs = local_rest(q[h], k[h], v[h], do[h], s0[h], rows[h], invs[h], pmat[h], gs[h])
            dq[h] = outs[0].astype(BF)
            z[h], ub[h], dk0[h], dg0[h] = outs[1:]

    def carry_batch(b):
        for j in range(size):

            @pl.when(rank != j)
            def _():
                send_back(b, rank, j).wait_recv()

        for j in range(size):
            h = j * own + b
            outs = carry_head(
                k[h], v[h], s0[h], ein[h], rows[h], ub[h], w0[h], nb[h], z[h], gram[h], gs[h],
                dk0[h], dg0[h],
            )
            dv[h] = outs[0].astype(BF)
            dk[h] = outs[1].astype(BF)
            dgs[pl.ds(h, 1), :] = outs[2]
            dbs[pl.ds(h, 1), :] = outs[3]

    late = max(own, planes) + 1

    def step(s):
        @pl.when(s < own)
        def _():
            local_batch(s)

            @pl.when(s == 0)
            def _():
                pl.semaphore_wait(barrier, n + m - 2)
                run(1, m, lambda d: send_weights(side_ahead(d), side).start())

            local_sends(s)

        turn = s - 1 - lag

        @pl.when((lag > 0) & (turn >= 0) & (turn < own))
        def _():
            hand_on(turn)

        @pl.when(s == own)
        def _():
            run(0, own, rest_batch)

        @pl.when((s >= 1) & (s <= own))
        def _():
            compose(s - 1)

            @pl.when(lag == 0)
            def _():
                hand_on(s - 1)

        @pl.when(s >= late)
        def _():
            carry_batch(s - late)

    run(0, own + late, step)

    row, col = indices(c)
    tri = jnp.where(row >= col, 1.0, 0.0).astype(BF)
    sums = mm(jnp.concatenate(split3(dgs[...]), axis=0), tri)
    dlog = sums[:heads] + sums[heads : 2 * heads] + sums[2 * heads :]
    grads = jnp.concatenate([dlog * fac[:heads], dbs[...] * fac[heads:]], axis=0).astype(BF)
    ggot[side] = grads
    run(1, m, lambda d: send_grads(side_ahead(d), side).start())
    width = hidden.shape[1]
    w = width // n
    terms = mm(grads, hidden[...])
    for i in range(n):
        tbuf[i] = terms[:, i * w : (i + 1) * w].astype(BF)
    run(1, n, lambda d: scatter(ahead(d), me).start())
    wgot[side] = weights[side]

    def partner(d):
        source = side_behind(d)
        send_weights(source, source).wait_recv()
        send_grads(source, source).wait_recv()

    run(1, m, partner)
    total = mm(ggot[0], wgot[0], 0, 0)
    for i in range(1, m):
        total = total + mm(ggot[i], wgot[i], 0, 0)
    gh[...] = total.astype(BF)

    def add(d, acc):
        source = behind(d)
        scatter(source, source).wait_recv()
        return acc + got[source].astype(F32)

    acc = lax.fori_loop(1, n, add, tbuf[me].astype(F32)).astype(BF)
    part[...] = acc
    gathered[me] = acc
    run(1, n, lambda d: gather(ahead(d), me).start())

    def arrive(d):
        source = behind(d)
        gather(source, source).wait_recv()

    run(1, n, arrive)
    for i in range(n):
        both = gathered[i].astype(F32)
        gd[:, i * w : (i + 1) * w] = both[:heads]
        gw[:, i * w : (i + 1) * w] = both[heads:]

    def done(b):
        for j in range(size):

            @pl.when(rank != j)
            def _():
                send_map(b, j, rank).wait_send()
                send_back(b, j, rank).wait_send()

        @pl.when(plane > 0)
        def _():
            send_plane(b).wait_send()

    run(0, own, done)
    run(1, n, lambda d: scatter(ahead(d), me).wait_send())
    run(1, n, lambda d: gather(ahead(d), me).wait_send())
    run(1, m, lambda d: send_weights(side_ahead(d), side).wait_send())
    run(1, m, lambda d: send_grads(side_ahead(d), side).wait_send())


def whole_part(n, m, q, k, v, do, s0, rows, fac, hidden, weights):
    h, c, dk = q.shape
    dv = v.shape[2]
    size = group_size(n, h)
    own = h // size
    width = hidden.shape[1]
    vm = pl.BlockSpec(memory_space=pltpu.VMEM)
    sd = jax.ShapeDtypeStruct
    dma = pltpu.SemaphoreType.DMA
    message = (2 * dk + 16, dv)
    return pl.pallas_call(
        partial(whole_kernel, n, m, size),
        out_shape=(
            sd((h, c, dk), BF), sd((h, c, dk), BF), sd((h, c, dv), BF), sd((c, width // m), BF),
            sd((h, width), F32), sd((h, width), F32),
        ),
        in_specs=[vm] * 9,
        out_specs=(vm,) * 6,
        scratch_shapes=[
            pltpu.VMEM((h, c, c), F32), pltpu.VMEM((h, c, c), F32), pltpu.VMEM((h, c, c), F32),
            pltpu.VMEM((h, c, c), BF), pltpu.VMEM((h, c, dv), F32), pltpu.VMEM((h, c, dk), BF),
            pltpu.VMEM((h, c, dv), F32), pltpu.VMEM((h, c, dv), BF), pltpu.VMEM((h, c, dk), F32),
            pltpu.VMEM((h, 1, c), F32), pltpu.VMEM((h, c), F32), pltpu.VMEM((h, c), F32),
            pltpu.VMEM((own, size) + message, BF), pltpu.VMEM((own, size) + message, BF),
            pltpu.VMEM((own, dk, dk), BF), pltpu.VMEM((own, dk, dv), F32),
            pltpu.VMEM((own, 8, dv), F32),
            pltpu.VMEM((own, dk, dv), BF), pltpu.VMEM((own, dk, dv), BF),
            pltpu.VMEM((own, size, dk, dv), BF), pltpu.VMEM((h, dk, dv), BF),
            pltpu.VMEM((n, 2 * h, width // n), BF), pltpu.VMEM((n, 2 * h, width // n), BF),
            pltpu.VMEM((2 * h, width // n), BF), pltpu.VMEM((n, 2 * h, width // n), BF),
            pltpu.VMEM((m, 2 * h, c), BF), pltpu.VMEM((m, 2 * h, width // m), BF),
            dma((own, size)), dma((own, size)), dma((2, own)), dma((own, size)), dma((h,)),
            dma((4, n)), dma((4, m)),
        ],
        compiler_params=pltpu.CompilerParams(
            collective_id=0, has_side_effects=True, vmem_limit_bytes=56 * 1024 * 1024
        ),
    )(q, k, v, do, s0, rows, fac, hidden, weights)


def gates(hidden_in, both, decay_bias, decay_log, write_bias):
    h = decay_bias.shape[0]
    logits = lax.dot_general(
        both, hidden_in, (((0,), (1,)), ((), ())), preferred_element_type=F32
    )
    pre = logits[:h] + decay_bias[:, None]
    rate = jnp.exp(decay_log)[:, None]
    beta = jax.nn.sigmoid(logits[h:] + write_bias[:, None])
    log_decay = -rate * jax.nn.softplus(pre)
    c = log_decay.shape[1]
    ones = jnp.triu(jnp.ones((c, c), F32))
    g = jnp.dot(log_decay, ones, precision=HI)
    return pre, rate, beta, g, ones


def shards(
    queries,
    key_vectors,
    values,
    out_grad,
    hidden_in,
    decay_weight,
    write_weight,
    decay_bias,
    decay_log,
    write_bias,
    start_state,
):
    n, m = lax.axis_size("seq"), lax.axis_size("head")
    both = jnp.concatenate([decay_weight, write_weight], axis=1)
    pre, rate, beta, g, _ = gates(hidden_in, both, decay_bias, decay_log, write_bias)
    h, c = g.shape
    rows = jnp.concatenate(
        [g[:, None], beta[:, None], jnp.zeros((h, 6, c), F32)], axis=1
    )
    fac = jnp.concatenate([-rate * jax.nn.sigmoid(pre), beta * (1.0 - beta)], axis=0)
    width = hidden_in.shape[1]
    weights = jnp.swapaxes(both.T.reshape(2 * h, m, width // m), 0, 1)
    q, k, v, do = (jnp.swapaxes(a, 0, 1) for a in (queries, key_vectors, values, out_grad))
    dq, dk, dv, gh, gd, gw = whole_part(
        n, m, q, k, v, do, start_state[0], rows, fac, hidden_in, weights
    )
    return (
        jnp.swapaxes(dq, 0, 1),
        jnp.swapaxes(dk, 0, 1),
        jnp.swapaxes(dv, 0, 1),
        gh,
        gd.T,
        gw.T,
    )


def solution(mesh):
    placed = (
        P("seq", "head", None),
        P("seq", "head", None),
        P("seq", "head", None),
        P("seq", "head", None),
        P("seq", None),
        P(None, "head"),
        P(None, "head"),
        P("head"),
        P("head"),
        P("head"),
        P("seq", "head", None, None),
    )
    return jax.shard_map(
        shards,
        mesh=mesh,
        in_specs=placed,
        out_specs=(
            P("seq", "head", None),
            P("seq", "head", None),
            P("seq", "head", None),
            P("seq", "head"),
            P(None, "head"),
            P(None, "head"),
        ),
        check_vma=False,
    )
```

time: 131 us -> 80.7 us (0.62)
  Pallas kernels: 111 us -> 64.7 us
  local copies, waits for them, and re-layouts: 16.6 us -> 12 us
    pallas_call x4 -> x1, Pallas kernels: 111 us -> 64.7 us  [whole_part(): pl.pallas_call(partial(whole_kernel, n, m, size), out_shape=(sd((h, c, dk...]
    unnamed x44 -> x33, local copies, waits for them, and re-layouts: 13.9 us -> 8.69 us
    transpose x2, local copies, waits for them, and re-layouts: 0.54 us -> 2.56 us  [shards(): jnp.swapaxes(a, 0, 1)]
    dot_general x3 -> x0, matrix products: 1.64 us -> none  [the longest x1 1.15 us: shards(): lax.dot_general(jnp.broadcast_to(grads, (m,) + grads.shape), both.reshape...]
    slice x2 -> x0, local copies, waits for them, and re-layouts: 1.33 us -> none  [the longest x1 0.66 us: shards(): total[h:]]
where the time goes in v1:
time: 80.7 us; the launch traced here: 80.4 us
  Pallas kernels  64.7 us (80%)
  local copies, waits for them, and re-layouts  12 us (15%)
  matrix products  1.63 us (2%)
  other arithmetic  1.42 us (2%)
    pallas_call x1, Pallas kernels, whole_part(): pl.pallas_call(partial(whole_kernel, n, m, size), out_shape=(sd((h, c, dk...  64.7 us
    unnamed x33, local copies, waits for them, and re-layouts  8.69 us
    transpose x2, local copies, waits for them, and re-layouts, shards(): jnp.swapaxes(a, 0, 1)  2.56 us

profile of v1, /device:TPU:0, one launch (start us, length us, event | category | flops | bytes accessed | tf_op | source)
XLA Modules:
  0.0 80.4 jit_solution(15876039030840525510)
XLA Ops:
  0.6 0.0 copy-start.12
  0.6 0.6 copy-done.12
  1.3 0.1 pad.4.clone
  1.4 0.0 copy-start.9
  1.4 0.9 %constant_dynamic-update-slice_fusion.1 = bf16[2048,32]{0,1:T(8,128)(2,1)S(1)} fusion(bf16[2048,16]{0,1:T(8,128)(2,1)} %param.16), kind=kLoop, calls=%fused_computation.30 | loop fusion | bytes 131072
  2.3 0.0 copy-done.9
  2.3 0.0 copy-start.11
  2.3 0.0 copy-start.10
  2.3 0.0 copy-start.2
  2.3 0.0 copy-start.3
  2.3 1.4 %fusion.23 = f32[32,128]{1,0:T(8,128)S(1)} fusion(bf16[2048,32]{0,1:T(8,128)(2,1)S(1)} %constant_dynamic-update-slice_fusion, bf16[128,2048]{1,0:T(8,128)(2,1)} %hidden.1), kind=kOutput, calls=%fused_computation.38 | convolution fusion | flops 16777216 | bytes 671744 | tf_op jit(solution)/shard_map/dot_general | solution.py:503
  3.7 0.0 copy-done.11
  3.7 0.2 fusion
  4.0 0.0 copy-done.10
  4.0 0.1 subtract_multiply_fusion
  4.1 0.6 pad_maximum_fusion.fac
  4.7 0.7 maximum_maximum_fusion.rows
  5.4 0.7 copy.40
  6.1 0.0 copy-done.2
  6.1 0.0 copy-done.3
  6.1 0.0 copy-start.4
  6.1 0.0 copy-start.5
  6.1 1.3 %copy_bitcast_fusion.2 = (bf16[16,128,128]{2,1,0:T(8,128)(2,1)}, bf16[16,128,128]{2,1,0:T(8,128)(2,1)}) fusion(bf16[128,16,128]{2,1,0:T(8,128)(2,1)S(1)} %copy-done.2, bf16[128,16,128]{2,1,0:T(8,128)(2,1)S(1)} %copy-done.3), kind=kLoop, calls=%fused_computation.2 | loop fusion | bytes 2097152 | tf_op jit(solution)/shard_map/transpose | solution.py:539
  7.4 0.0 copy-done.4
  7.4 0.0 copy-done.5
  7.4 1.3 %copy_bitcast_fusion = (bf16[16,128,128]{2,1,0:T(8,128)(2,1)}, bf16[16,128,128]{2,1,0:T(8,128)(2,1)}) fusion(bf16[128,16,128]{2,1,0:T(8,128)(2,1)S(1)} %copy-done.4, bf16[128,16,128]{2,1,0:T(8,128)(2,1)S(1)} %copy-done.5), kind=kLoop, calls=%fused_computation | loop fusion | bytes 2097152 | tf_op jit(solution)/shard_map/transpose | solution.py:539
  8.6 64.7 %shard_map.154 = (bf16[16,128,128]{2,1,0:T(8,128)(2,1)}, bf16[16,128,128]{2,1,0:T(8,128)(2,1)}, bf16[16,128,128]{2,1,0:T(8,128)(2,1)}, bf16[128,1024]{1,0:T(8,12...) custom-call(bf16[16,128,128]{2,1,0:T(8,128)(2,1)} %get-tuple-element.36.q, bf16[16,128,128]{2,1,0:T(8,128)(2,1)} %get-tuple-element.35.k, ...), custom_call_target="tpu_custom_call" | custom-call | tf_op jit(solution)/shard_map/pallas_call | solution.py:471
  73.3 0.0 copy-start.1
  73.3 2.2 %copy.31 = bf16[128,16,128]{2,1,0:T(8,128)(2,1)} copy(bf16[128,16,128]{2,0,1:T(8,128)(2,1)} %bitcast.32) | data formatting | bytes 1048576
  75.6 0.0 copy-done.1
  75.6 0.0 copy-start
  75.6 1.1 %copy.32 = bf16[128,16,128]{2,1,0:T(8,128)(2,1)} copy(bf16[128,16,128]{2,0,1:T(8,128)(2,1)S(1)} %bitcast.31) | data formatting | bytes 1048576
  76.7 0.0 copy-done
  76.7 0.0 copy-start.6
  76.7 1.1 %copy.33 = bf16[128,16,128]{2,1,0:T(8,128)(2,1)} copy(bf16[128,16,128]{2,0,1:T(8,128)(2,1)S(1)} %bitcast.30) | data formatting | bytes 1048576
  77.8 0.0 copy-done.6
  77.8 0.0 copy-start.8
  77.8 0.7 copy.45
  78.5 0.3 copy-done.8
  78.8 0.0 copy-start.7
  78.8 0.7 copy.46
  79.5 0.3 copy-done.7
  79.8 0.7 copy.47
  (4 shorter events, 0.0 us)
Async XLA Ops:
  0.6 0.7 copy-start.12
  1.4 0.9 %copy-start.9 = (bf16[2048,16]{0,1:T(8,128)(2,1)S(1)}, bf16[2048,16]{0,1:T(8,128)(2,1)}, u32[]{:S(2)}) copy-start(bf16[2048,16]{0,1:T(8,128)(2,1)} %param.17) | copy-start | bytes 196612
  2.3 1.5 %copy-start.11 = (f32[16]{0:T(128)S(1)}, f32[16]{0:T(128)}, u32[]{:S(2)}) copy-start(f32[16]{0:T(128)} %param.18) | copy-start | bytes 196
  2.3 1.7 %copy-start.10 = (f32[16]{0:T(128)S(1)}, f32[16]{0:T(128)}, u32[]{:S(2)}) copy-start(f32[16]{0:T(128)} %param.20) | copy-start | bytes 196
  2.3 3.8 %copy-start.2 = (bf16[128,16,128]{2,1,0:T(8,128)(2,1)S(1)}, bf16[128,16,128]{2,1,0:T(8,128)(2,1)}, u32[]{:S(2)}) copy-start(bf16[128,16,128]{2,1,0:T(8,128)(2,1)} %param.12) | copy-start | bytes 1572868
  2.3 3.8 %copy-start.3 = (bf16[128,16,128]{2,1,0:T(8,128)(2,1)S(1)}, bf16[128,16,128]{2,1,0:T(8,128)(2,1)}, u32[]{:S(2)}) copy-start(bf16[128,16,128]{2,1,0:T(8,128)(2,1)} %param.11) | copy-start | bytes 1572868
  6.1 1.3 %copy-start.4 = (bf16[128,16,128]{2,1,0:T(8,128)(2,1)S(1)}, bf16[128,16,128]{2,1,0:T(8,128)(2,1)}, u32[]{:S(2)}) copy-start(bf16[128,16,128]{2,1,0:T(8,128)(2,1)} %param.14) | copy-start | bytes 1572868
  6.1 1.3 %copy-start.5 = (bf16[128,16,128]{2,1,0:T(8,128)(2,1)S(1)}, bf16[128,16,128]{2,1,0:T(8,128)(2,1)}, u32[]{:S(2)}) copy-start(bf16[128,16,128]{2,1,0:T(8,128)(2,1)} %param.13) | copy-start | bytes 1572868
  73.3 2.2 %copy-start.1 = (bf16[16,128,128]{2,1,0:T(8,128)(2,1)S(1)}, bf16[16,128,128]{2,1,0:T(8,128)(2,1)}, u32[]{:S(2)}) copy-start(bf16[16,128,128]{2,1,0:T(8,128)(2,1)} %get-tuple-element.13) | copy-start | bytes 1572868
  75.6 1.1 %copy-start = (bf16[16,128,128]{2,1,0:T(8,128)(2,1)S(1)}, bf16[16,128,128]{2,1,0:T(8,128)(2,1)}, u32[]{:S(2)}) copy-start(bf16[16,128,128]{2,1,0:T(8,128)(2,1)} %get-tuple-element.14) | copy-start | bytes 1572868
  76.7 1.1 %copy-start.6 = (bf16[128,1024]{1,0:T(8,128)(2,1)S(1)}, bf16[128,1024]{1,0:T(8,128)(2,1)}, u32[]{:S(2)}) copy-start(bf16[128,1024]{1,0:T(8,128)(2,1)} %get-tuple-element.46) | copy-start | bytes 786436
  77.8 1.0 %copy-start.8 = (f32[16,2048]{1,0:T(8,128)S(1)}, f32[16,2048]{1,0:T(8,128)}, u32[]{:S(2)}) copy-start(f32[16,2048]{1,0:T(8,128)} %get-tuple-element.16) | copy-start | bytes 393220
  78.8 1.0 %copy-start.7 = (f32[16,2048]{1,0:T(8,128)S(1)}, f32[16,2048]{1,0:T(8,128)}, u32[]{:S(2)}) copy-start(f32[16,2048]{1,0:T(8,128)} %get-tuple-element.17) | copy-start | bytes 393220

commit v2 on v1

v2 whole, which is shorter than its diff:
```python
from functools import partial

import jax
import jax.numpy as jnp
from jax import lax
from jax.experimental import pallas as pl
from jax.experimental.pallas import tpu as pltpu
from jax.sharding import PartitionSpec as P

EPSILON = 1e-06
F32 = jnp.float32
BF = jnp.bfloat16


def mm(a, b, ca=1, cb=0):
    return lax.dot_general(
        a.astype(BF), b.astype(BF), (((ca,), (cb,)), ((), ())), preferred_element_type=F32
    )


def indices(c):
    row = lax.broadcasted_iota(jnp.int32, (c, c), 0)
    col = lax.broadcasted_iota(jnp.int32, (c, c), 1)
    return row, col


def inverses(couplings):
    c = couplings[0].shape[0]
    row, col = indices(c)
    invs = [
        jnp.where(row == col, 1.0, jnp.where((row ^ col) == 1, -a, 0.0)) for a in couplings
    ]
    level = 1
    while (2 << level) <= c:
        near = ((row >> level) ^ (col >> level)) == 1
        halves = [mm(x, jnp.where(near, a, 0.0)) for x, a in zip(invs, couplings)]
        invs = [x - mm(y, x) for x, y in zip(invs, halves)]
        level += 1
    return invs


def head_masks(c):
    row, col = indices(c)
    return row == col, col >= row, col > row


def down(x):
    return jnp.sum(x, axis=0, keepdims=True)


def to_col(eye, row):
    return jnp.sum(jnp.where(eye, row, 0.0), axis=1, keepdims=True)


def to_row(eye, x):
    return down(jnp.where(eye, jnp.sum(x, axis=1, keepdims=True), 0.0))


def scale_of(x):
    return lax.rsqrt(down(x * x) + EPSILON)


def local_first(q, k, rows):
    c = q.shape[0]
    eye, upper, strict = head_masks(c)
    g, beta = rows[0:1], rows[1:2]
    qt, kt = q.T, k.T
    rq, rk = scale_of(qt.astype(F32)), scale_of(kt.astype(F32))
    start = to_col(eye, jnp.log(rk) - g)
    decay = jnp.exp(jnp.where(upper, start + g, -1e30))
    grams = mm(k, jnp.concatenate([k, q], axis=0), 1, 1)
    kk = grams[:, :c]
    pt = decay * rq * grams[:, c:]
    pairs = jnp.where(strict, decay, 0.0) * rk
    return qt, kt, rq, rk, decay, pairs, kk, pt, beta * pairs * kk


def local_map(k, do, rows, inv, first):
    qt, kt, rq, rk, decay, pairs, kk, pt, a = first
    beta, cd, to_end = rows[1:2], rows[2:3], rows[3:4]
    dv = do.shape[1]
    ptdo = mm(pt, do).astype(BF)
    left = jnp.concatenate([inv.astype(BF), (inv * (to_end * rk)).astype(BF)], axis=1)
    right = jnp.concatenate(
        [
            jnp.concatenate([ptdo, jnp.zeros(k.shape, BF)], axis=1),
            jnp.concatenate([jnp.zeros(do.shape, BF), k], axis=1),
        ],
        axis=0,
    )
    both = mm(left, right)
    left = jnp.concatenate(
        [(qt * (cd * rq)).astype(BF), (kt * (-beta * cd * rk)).astype(BF)], axis=1
    )
    right = jnp.concatenate(
        [jnp.concatenate([do, jnp.zeros(k.shape, BF)], axis=1), both.astype(BF)], axis=0
    )
    return both[:, :dv], both[:, dv:], mm(left, right)


def local_rest(k, v, do, s0, rows, qt, kt, rq, rk, decay, pt, inv):
    c = k.shape[0]
    eye, _, _ = head_masks(c)
    beta, cd = rows[1:2], rows[2:3]
    sb = s0.astype(BF)
    ks = mm(k, sb)
    back = inv.T
    left = jnp.concatenate([back * beta, back * (-beta * cd * rk)], axis=1)
    ub = mm(left, jnp.concatenate([v, ks.astype(BF)], axis=0)).astype(BF)
    prod = mm(jnp.concatenate([ub, sb], axis=0), do, 1, 1)
    dpt, dost = prod[:c], prod[c:] * cd
    t = dpt * pt
    gdp = (decay * dpt).astype(BF)
    qn = qt * rq
    dqn = rq * (dost + mm(kt, gdp))
    dq = dqn - qn * down(qn * dqn)
    dk0 = mm(qn, gdp, 1, 1)
    dg0 = down(t) + down(dost * qn) - to_row(eye, t)
    return dq.astype(BF).T, ks, ub, dk0, dg0


def carry_head(v, s0, e, rows, kt, rk, pairs, kk, ub, w0, nb, ks, dk0, dg0):
    c = v.shape[0]
    eye, _, _ = head_masks(c)
    beta, cd, to_end = rows[1:2], rows[2:3], rows[3:4]
    w = w0 + mm(nb, e)
    wb = w.astype(BF)
    dv = to_col(eye, beta) * w
    prod = mm(jnp.concatenate([ub, s0.astype(BF)], axis=0), wb, 1, 1)
    da = -prod[:c] * pairs
    ue = (to_end * rk) * mm(e, ub, 1, 1)
    pair = (beta * da).astype(BF)
    kn = kt * rk
    dkn = dk0 - (beta * cd * rk) * prod[c:] + mm(kt, pair) + mm(kt, pair, 1, 1) + ue
    dk = dkn - kn * down(kn * dkn)
    da = da * kk
    own = down(da)
    wks = (cd * rk) * to_row(eye, w * ks)
    dbeta = own + to_row(eye, w * v.astype(F32)) - wks
    s = down(kt * ue)
    dg = dg0 + beta * (own - wks) - to_row(eye, beta * da) - s
    last = cd[:, c - 1 :]
    tail = jnp.sum(s, keepdims=True) + last * jnp.sum(down(s0 * e.astype(F32)), keepdims=True)
    lane = lax.broadcasted_iota(jnp.int32, (1, c), 1)
    dg = dg + jnp.where(lane == c - 1, tail, 0.0)
    return dv, dk.astype(BF).T, dg, dbeta


def split3(x):
    hi = x.astype(BF)
    rest = x - hi.astype(F32)
    mid = rest.astype(BF)
    return hi, mid, (rest - mid.astype(F32)).astype(BF)


def group_size(n, heads):
    size = 1
    while (2 * size) ** 2 <= n and heads % (2 * size) == 0 and n % (2 * size) == 0:
        size *= 2
    return size


def whole_kernel(
    n, m, size,
    q, k, v, do, s0, hidden, decay_w, write_w, decay_bias, decay_log, write_bias,
    dq, dk, dv, gh, gd, gw,
    rows, fac, weights, qts, kts, scales, decay, pairs, kks, pts, invs, w0, nb, ks, ub, dk0, dg0, dgs, dbs,
    maps, maps_in, tcomp, bcomp, gcomp, zin, zout, eout, ein,
    tbuf, got, part, gathered, ggot, wgot,
    map_sems, map_recv, z_sems, e_send, e_recv, sum_sems, head_sems,
):
    me, side = lax.axis_index("seq"), lax.axis_index("head")
    mesh_id = pl.DeviceIdType.MESH
    heads, c, dkk = q.shape
    dvv = v.shape[2]
    own = heads // size
    planes = n // size
    plane, rank = me // size, lax.rem(me, size)
    lag = planes - 1 - plane
    barrier = pltpu.get_barrier_semaphore()

    def run(low, high, body):
        def step(d, _):
            body(d)
            return 0

        lax.fori_loop(low, high, step, 0)

    def ahead(d):
        return lax.rem(me + d, n)

    def behind(d):
        return lax.rem(me + n - d, n)

    def side_ahead(d):
        return lax.rem(side + d, m)

    def side_behind(d):
        return lax.rem(side + m - d, m)

    def greet(d):
        pl.semaphore_signal(barrier, inc=1, device_id={"seq": ahead(d)}, device_id_type=mesh_id)

    def greet_side(d):
        pl.semaphore_signal(
            barrier, inc=1, device_id={"head": side_ahead(d)}, device_id_type=mesh_id
        )

    run(1, n, greet)
    run(1, m, greet_side)
    width = hidden.shape[1]
    w = width // n

    def send_map(b, to, source):
        return pltpu.make_async_remote_copy(
            src_ref=maps.at[b, to], dst_ref=maps_in.at[b, source],
            send_sem=map_sems.at[b, to], recv_sem=map_recv.at[b, source],
            device_id={"seq": plane * size + to}, device_id_type=mesh_id,
        )

    def send_plane(b):
        return pltpu.make_async_remote_copy(
            src_ref=zout.at[b], dst_ref=zin.at[b],
            send_sem=z_sems.at[0, b], recv_sem=z_sems.at[1, b],
            device_id={"seq": lax.rem(me + n - size, n)}, device_id_type=mesh_id,
        )

    def send_back(b, to, owner):
        return pltpu.make_async_remote_copy(
            src_ref=eout.at[b, to], dst_ref=ein.at[owner * own + b],
            send_sem=e_send.at[b, to], recv_sem=e_recv.at[owner * own + b],
            device_id={"seq": plane * size + to}, device_id_type=mesh_id,
        )

    def scatter(to, source):
        return pltpu.make_async_remote_copy(
            src_ref=tbuf.at[to], dst_ref=got.at[source],
            send_sem=sum_sems.at[0, to], recv_sem=sum_sems.at[1, source],
            device_id={"seq": to}, device_id_type=mesh_id,
        )

    def gather(to, source):
        return pltpu.make_async_remote_copy(
            src_ref=part, dst_ref=gathered.at[source],
            send_sem=sum_sems.at[2, to], recv_sem=sum_sems.at[3, source],
            device_id={"seq": to}, device_id_type=mesh_id,
        )

    def send_weights(to, source):
        return pltpu.make_async_remote_copy(
            src_ref=weights.at[to], dst_ref=wgot.at[source],
            send_sem=head_sems.at[0, to], recv_sem=head_sems.at[1, source],
            device_id={"head": to}, device_id_type=mesh_id,
        )

    def send_grads(to, source):
        return pltpu.make_async_remote_copy(
            src_ref=ggot.at[side], dst_ref=ggot.at[source],
            send_sem=head_sems.at[2, to], recv_sem=head_sems.at[3, source],
            device_id={"head": to}, device_id_type=mesh_id,
        )

    @pl.when(lag == 0)
    def _():
        zin[...] = jnp.zeros(zin.shape, BF)

    def prepare():
        eye = head_masks(heads)[0]
        for i in range(m):
            cut = pl.ds(i * (width // m), width // m)
            weights[i] = jnp.concatenate([decay_w[:, cut], write_w[:, cut]], axis=0)
        logits = mm(jnp.concatenate([decay_w[...], write_w[...]], axis=0), hidden[...], 1, 1)
        pre = logits[:heads] + to_col(eye, decay_bias[...])
        rate = jnp.exp(to_col(eye, decay_log[...]))
        beta = jax.nn.sigmoid(logits[heads:] + to_col(eye, write_bias[...]))
        log_decay = -rate * (jnp.maximum(pre, 0.0) + jnp.log1p(jnp.exp(-jnp.abs(pre))))
        row, col = indices(c)
        tri = jnp.where(row <= col, 1.0, 0.0).astype(BF)
        sums = mm(jnp.concatenate(split3(log_decay), axis=0), tri)
        g = sums[:heads] + sums[heads : 2 * heads] + sums[2 * heads :]
        fac[:heads] = -rate * jax.nn.sigmoid(pre)
        fac[heads:] = beta * (1.0 - beta)
        parts = (g, beta, jnp.exp(g), jnp.exp(g[:, c - 1 :] - g))
        for h in range(heads):
            for i, a in enumerate(parts):
                rows[h, i : i + 1] = a[h : h + 1]

    def wait_barrier():
        pl.semaphore_wait(barrier, n + m - 2)

    def local_batch(b):
        hs = [j * own + b for j in range(size)]
        firsts = [local_first(q[h], k[h], rows[h]) for h in hs]
        solved = inverses([first[8] for first in firsts])
        messages = []
        for j, h in enumerate(hs):
            qt, kt, rq, rk, decay_, pairs_, kk, pt, _ = firsts[j]
            w0_, nb_, made = local_map(k[h], do[h], rows[h], solved[j], firsts[j])
            qts[h], kts[h] = qt, kt
            scales[h, 0:1] = rq
            scales[h, 1:2] = rk
            decay[h], pairs[h], kks[h], pts[h] = decay_, pairs_, kk, pt
            invs[h], w0[h], nb[h] = solved[j].astype(BF), w0_, nb_.astype(BF)
            last = jnp.broadcast_to(rows[h][2:3, c - 1 :], (8, dvv + dkk))
            high = last.astype(BF)
            low = (last - high.astype(F32)).astype(BF)
            messages.append(jnp.concatenate([made.astype(BF), high, low], axis=0))
            maps[b, j] = messages[j]

        for j in range(size):

            @pl.when(rank == j)
            def _():
                maps_in[b, j] = messages[j]

    def local_sends(b):
        for j in range(size):

            @pl.when(rank != j)
            def _():
                send_map(b, j, rank).start()

    def piece(b, p):
        made = maps_in[b, p, :dkk]
        ends = maps_in[b, p, dkk:].astype(F32)
        return made, ends[0:1] + ends[8:9]

    def wait_maps(b):
        for p in range(size):

            @pl.when(rank != p)
            def _():
                send_map(b, p, p).wait_recv()

    def compose(b):
        wait_maps(b)
        made, g = piece(b, size - 1)
        both = made.astype(F32)
        for p in range(size - 2, -1, -1):
            made, last = piece(b, p)
            step = made.astype(F32)
            prod = mm(made[:, dvv:], both)
            both = last * both + jnp.concatenate(
                [step[:, :dvv], g[:, dvv:] * step[:, dvv:]], axis=1
            ) + prod
            g = last * g
        bcomp[b] = both[:, :dvv]
        tcomp[b] = both[:, dvv:].astype(BF)
        gcomp[b] = jnp.broadcast_to(g[:, :dvv], gcomp.shape[1:])

    def wait_plane(b):
        @pl.when(lag > 0)
        def _():
            send_plane(b).wait_recv()

    def hand_on(b):
        wait_plane(b)
        eb = zin[b]

        @pl.when(plane > 0)
        def _():
            e = gcomp[b, 0:1] * eb.astype(F32) + bcomp[b] + mm(tcomp[b], eb)
            zout[b] = e.astype(BF)
            send_plane(b).start()

        e = eb.astype(F32)
        for p in range(size - 1, -1, -1):
            eout[b, p] = eb

            @pl.when(rank == p)
            def _():
                ein[rank * own + b] = eb

            @pl.when(rank != p)
            def _():
                send_back(b, p, rank).start()

            if p > 0:
                made, last = piece(b, p)
                e = last[:, :dvv] * e + made[:, :dvv].astype(F32) + mm(made[:, dvv:], eb)
                eb = e.astype(BF)

    def rest_batch(b):
        for j in range(size):
            h = j * own + b
            dq[h], ks[h], ub[h], dk0[h], dg0[h] = local_rest(
                k[h], v[h], do[h], s0[h], rows[h], qts[h], kts[h],
                scales[h, 0:1], scales[h, 1:2], decay[h], pts[h], invs[h],
            )

    def wait_back(b):
        for j in range(size):

            @pl.when(rank != j)
            def _():
                send_back(b, rank, j).wait_recv()

    def carry_batch(b):
        wait_back(b)
        for j in range(size):
            h = j * own + b
            outs = carry_head(
                v[h], s0[h], ein[h], rows[h], kts[h], scales[h, 1:2], pairs[h], kks[h], ub[h],
                w0[h], nb[h], ks[h], dk0[h], dg0[h],
            )
            dv[h] = outs[0].astype(BF)
            dk[h] = outs[1]
            dgs[pl.ds(h, 1), :] = outs[2]
            dbs[pl.ds(h, 1), :] = outs[3]

    late = max(own, planes) + 1
    half = (own + 1) // 2

    def step(s):
        @pl.when(s < own)
        def _():
            local_batch(s)

            @pl.when(s == 0)
            def _():
                wait_barrier()
                run(1, m, lambda d: send_weights(side_ahead(d), side).start())

            local_sends(s)

        turn = s - 1 - lag

        @pl.when((lag > 0) & (turn >= 0) & (turn < own))
        def _():
            hand_on(turn)

        @pl.when(s == own)
        def _():
            run(0, half, rest_batch)

        @pl.when((s >= 1) & (s <= own))
        def _():
            compose(s - 1)

            @pl.when(lag == 0)
            def _():
                hand_on(s - 1)

        @pl.when((s > own) & (s < 2 * own + 1 - half))
        def _():
            rest_batch(s - own - 1 + half)

        @pl.when(s >= late)
        def _():
            carry_batch(s - late)

    prepare()
    run(0, own + late, step)

    def finish_grads():
        row, col = indices(c)
        tri = jnp.where(row >= col, 1.0, 0.0).astype(BF)
        sums = mm(jnp.concatenate(split3(dgs[...]), axis=0), tri)
        dlog = sums[:heads] + sums[heads : 2 * heads] + sums[2 * heads :]
        grads = jnp.concatenate([dlog * fac[:heads], dbs[...] * fac[heads:]], axis=0).astype(BF)
        ggot[side] = grads
        run(1, m, lambda d: send_grads(side_ahead(d), side).start())
        return grads

    def weight_terms(grads):
        terms = mm(grads, hidden[...])
        for i in range(n):
            tbuf[i] = terms[:, i * w : (i + 1) * w].astype(BF)
        run(1, n, lambda d: scatter(ahead(d), me).start())

    def partner(d):
        source = side_behind(d)
        send_weights(source, source).wait_recv()
        send_grads(source, source).wait_recv()

    def input_grad():
        wgot[side] = weights[side]
        run(1, m, partner)
        total = mm(ggot[0], wgot[0], 0, 0)
        for i in range(1, m):
            total = total + mm(ggot[i], wgot[i], 0, 0)
        gh[...] = total.astype(BF)

    def reduce_terms():
        def add(d, acc):
            source = behind(d)
            scatter(source, source).wait_recv()
            return acc + got[source].astype(F32)

        acc = lax.fori_loop(1, n, add, tbuf[me].astype(F32)).astype(BF)
        part[...] = acc
        gathered[me] = acc
        run(1, n, lambda d: gather(ahead(d), me).start())

    def arrive(d):
        source = behind(d)
        gather(source, source).wait_recv()

    def arrivals():
        run(1, n, arrive)

    def write_sums():
        for i in range(n):
            both = gathered[i].astype(F32)
            gd[:, i * w : (i + 1) * w] = both[:heads]
            gw[:, i * w : (i + 1) * w] = both[heads:]

    def done(b):
        for j in range(size):

            @pl.when(rank != j)
            def _():
                send_map(b, j, rank).wait_send()
                send_back(b, j, rank).wait_send()

        @pl.when(plane > 0)
        def _():
            send_plane(b).wait_send()

    weight_terms(finish_grads())
    input_grad()
    reduce_terms()
    arrivals()
    write_sums()
    run(0, own, done)
    run(1, n, lambda d: scatter(ahead(d), me).wait_send())
    run(1, n, lambda d: gather(ahead(d), me).wait_send())
    run(1, m, lambda d: send_weights(side_ahead(d), side).wait_send())
    run(1, m, lambda d: send_grads(side_ahead(d), side).wait_send())


def whole_part(n, m, q, k, v, do, s0, hidden, *gates):
    h, c, dk = q.shape
    dv = v.shape[2]
    size = group_size(n, h)
    own = h // size
    width = hidden.shape[1]
    vm = pl.BlockSpec(memory_space=pltpu.VMEM)
    sd = jax.ShapeDtypeStruct
    dma = pltpu.SemaphoreType.DMA
    message = (dk + 16, dv + dk)
    return pl.pallas_call(
        partial(whole_kernel, n, m, size),
        out_shape=(
            sd((h, c, dk), BF), sd((h, c, dk), BF), sd((h, c, dv), BF), sd((c, width // m), BF),
            sd((h, width), F32), sd((h, width), F32),
        ),
        in_specs=[vm] * 11,
        out_specs=(vm,) * 6,
        scratch_shapes=[
            pltpu.VMEM((h, 8, c), F32), pltpu.VMEM((2 * h, c), F32),
            pltpu.VMEM((m, 2 * h, width // m), BF),
            pltpu.VMEM((h, dk, c), BF), pltpu.VMEM((h, dk, c), BF), pltpu.VMEM((h, 8, c), F32),
            pltpu.VMEM((h, c, c), F32), pltpu.VMEM((h, c, c), F32), pltpu.VMEM((h, c, c), F32),
            pltpu.VMEM((h, c, c), F32), pltpu.VMEM((h, c, c), BF), pltpu.VMEM((h, c, dv), F32),
            pltpu.VMEM((h, c, dk), BF), pltpu.VMEM((h, c, dv), F32), pltpu.VMEM((h, c, dv), BF),
            pltpu.VMEM((h, dk, c), F32),
            pltpu.VMEM((h, 1, c), F32), pltpu.VMEM((h, c), F32), pltpu.VMEM((h, c), F32),
            pltpu.VMEM((own, size) + message, BF), pltpu.VMEM((own, size) + message, BF),
            pltpu.VMEM((own, dk, dk), BF), pltpu.VMEM((own, dk, dv), F32),
            pltpu.VMEM((own, 8, dv), F32),
            pltpu.VMEM((own, dk, dv), BF), pltpu.VMEM((own, dk, dv), BF),
            pltpu.VMEM((own, size, dk, dv), BF), pltpu.VMEM((h, dk, dv), BF),
            pltpu.VMEM((n, 2 * h, width // n), BF), pltpu.VMEM((n, 2 * h, width // n), BF),
            pltpu.VMEM((2 * h, width // n), BF), pltpu.VMEM((n, 2 * h, width // n), BF),
            pltpu.VMEM((m, 2 * h, c), BF), pltpu.VMEM((m, 2 * h, width // m), BF),
            dma((own, size)), dma((own, size)), dma((2, own)), dma((own, size)), dma((h,)),
            dma((4, n)), dma((4, m)),
        ],
        compiler_params=pltpu.CompilerParams(
            collective_id=0, has_side_effects=True, vmem_limit_bytes=28 * 1024 * 1024
        ),
    )(q, k, v, do, s0, hidden, *gates)


def shards(
    queries,
    key_vectors,
    values,
    out_grad,
    hidden_in,
    decay_weight,
    write_weight,
    decay_bias,
    decay_log,
    write_bias,
    start_state,
):
    n, m = lax.axis_size("seq"), lax.axis_size("head")
    q, k, v, do = (jnp.swapaxes(a, 0, 1) for a in (queries, key_vectors, values, out_grad))
    dq, dk, dv, gh, gd, gw = whole_part(
        n, m, q, k, v, do, start_state[0], hidden_in, decay_weight.T, write_weight.T,
        decay_bias[None], decay_log[None], write_bias[None],
    )
    return (
        jnp.swapaxes(dq, 0, 1),
        jnp.swapaxes(dk, 0, 1),
        jnp.swapaxes(dv, 0, 1),
        gh,
        gd.T,
        gw.T,
    )


def solution(mesh):
    placed = (
        P("seq", "head", None),
        P("seq", "head", None),
        P("seq", "head", None),
        P("seq", "head", None),
        P("seq", None),
        P(None, "head"),
        P(None, "head"),
        P("head"),
        P("head"),
        P("head"),
        P("seq", "head", None, None),
    )
    return jax.shard_map(
        shards,
        mesh=mesh,
        in_specs=placed,
        out_specs=(
            P("seq", "head", None),
            P("seq", "head", None),
            P("seq", "head", None),
            P("seq", "head"),
            P(None, "head"),
            P(None, "head"),
        ),
        check_vma=False,
    )
```

time: 80.7 us -> 63.5 us (0.79)
  Pallas kernels: 64.7 us -> 54.3 us
  local copies, waits for them, and re-layouts: 12 us -> 8.29 us
  matrix products: 1.63 us -> 0 us
  other arithmetic: 1.42 us -> 0 us
    pallas_call x1, Pallas kernels: 64.7 us -> 54.3 us  [whole_part(): pl.pallas_call(partial(whole_kernel, n, m, size), out_shape=(sd((h, c, dk...]
    unnamed x33 -> x24, local copies, waits for them, and re-layouts: 8.69 us -> 6.46 us
    dot_general x2 -> x0, matrix products: 1.63 us -> none  [the longest x1 1.4 us: gates(): lax.dot_general(both, hidden_in, (((0,), (1,)), ((), ())), preferred_elem...]
    concatenate x2 -> x0, other arithmetic: 1.31 us -> none  [the longest x1 0.7 us: shards(): jnp.concatenate([g[:, None], beta[:, None], jnp.zeros((h, 6, c), F32)], a...]
where the time goes in v2:
time: 63.5 us; the launch traced here: 63.3 us
  Pallas kernels  54.3 us (86%)
  local copies, waits for them, and re-layouts  8.29 us (13%)
  between operations  0.75 us (1%)
    pallas_call x1, Pallas kernels, whole_part(): pl.pallas_call(partial(whole_kernel, n, m, size), out_shape=(sd((h, c, dk...  54.3 us
    unnamed x24, local copies, waits for them, and re-layouts  6.46 us
    transpose x2, local copies, waits for them, and re-layouts, shards(): jnp.swapaxes(a, 0, 1)  1.83 us

profile of v2, /device:TPU:0, one launch (start us, length us, event | category | flops | bytes accessed | tf_op | source)
XLA Modules:
  0.0 63.3 jit_solution(15494599626852925605)
XLA Ops:
  0.6 0.0 copy-start.7
  0.6 0.0 copy-start.8
  0.7 1.6 %copy_bitcast_fusion.2 = (bf16[16,128,128]{2,1,0:T(8,128)(2,1)S(1)}, bf16[16,128,128]{2,1,0:T(8,128)(2,1)S(1)}) fusion(bf16[128,16,128]{2,1,0:T(8,128)(2,1)} %param.12, bf16[128,16,128]{2,1,0:T(8,128)(2,1)} %param.11), kind=kLoop, calls=%fused_computation.2 | loop fusion | bytes 2097152 | tf_op jit(solution)/shard_map/transpose | solution.py:590
  2.2 0.0 copy-done.7
  2.2 0.0 copy-done.8
  2.2 0.0 copy-start
  2.2 0.0 copy-start.1
  2.3 0.0 copy-start.2
  2.3 0.0 copy-start.3
  2.3 0.3 copy_bitcast_fusion
  2.6 0.0 copy-start.4
  2.6 0.0 copy-start.5
  2.6 0.0 copy-start.6
  2.6 0.9 %copy-done = f32[1,16,128,128]{3,2,1,0:T(8,128)S(1)} copy-done((f32[1,16,128,128]{3,2,1,0:T(8,128)S(1)}, f32[1,16,128,128]{3,2,1,0:T(8,128)}, u32[]{:S(2)}) %copy-start) | copy-done | bytes 1048600
  3.5 0.1 copy-done.1
  3.6 0.0 copy-done.2
  3.6 0.0 copy-done.3
  3.6 0.0 copy-done.4
  3.6 0.0 copy-done.5
  3.6 0.0 copy-done.6
  3.6 54.3 %shard_map.154 = (bf16[16,128,128]{2,1,0:T(8,128)(2,1)S(1)}, bf16[16,128,128]{2,1,0:T(8,128)(2,1)S(1)}, bf16[16,128,128]{2,1,0:T(8,128)(2,1)S(1)}, bf16[128,1024...) custom-call(bf16[16,128,128]{2,1,0:T(8,128)(2,1)S(1)} %get-tuple-element.27.q, ...), custom_call_target="tpu_custom_call" | custom-call | tf_op jit(solution)/shard_map/pallas_call | solution.py:542
  57.9 1.1 %copy.21 = bf16[128,16,128]{2,1,0:T(8,128)(2,1)} copy(bf16[128,16,128]{2,0,1:T(8,128)(2,1)S(1)} %bitcast.22) | data formatting | bytes 1048576
  59.1 1.1 %copy.22 = bf16[128,16,128]{2,1,0:T(8,128)(2,1)} copy(bf16[128,16,128]{2,0,1:T(8,128)(2,1)S(1)} %bitcast.21) | data formatting | bytes 1048576
  60.2 1.1 %copy.23 = bf16[128,16,128]{2,1,0:T(8,128)(2,1)} copy(bf16[128,16,128]{2,0,1:T(8,128)(2,1)S(1)} %bitcast.20) | data formatting | bytes 1048576
  61.3 0.7 %copy.31 = bf16[128,1024]{1,0:T(8,128)(2,1)} copy(bf16[128,1024]{1,0:T(8,128)(2,1)S(1)} %get-tuple-element.37) | data formatting | bytes 524288
  62.0 0.7 %copy.32 = f32[2048,16]{0,1:T(8,128)} copy(f32[2048,16]{0,1:T(8,128)S(1)} %bitcast.24) | data formatting | bytes 262144
  62.7 0.7 %copy.33 = f32[2048,16]{0,1:T(8,128)} copy(f32[2048,16]{0,1:T(8,128)S(1)} %bitcast.23) | data formatting | bytes 262144
Async XLA Ops:
  0.6 1.6 %copy-start.7 = (bf16[128,16,128]{2,1,0:T(8,128)(2,1)S(1)}, bf16[128,16,128]{2,1,0:T(8,128)(2,1)}, u32[]{:S(2)}) copy-start(bf16[128,16,128]{2,1,0:T(8,128)(2,1)} %param.14) | copy-start | bytes 1572868
  0.6 1.6 %copy-start.8 = (bf16[128,16,128]{2,1,0:T(8,128)(2,1)S(1)}, bf16[128,16,128]{2,1,0:T(8,128)(2,1)}, u32[]{:S(2)}) copy-start(bf16[128,16,128]{2,1,0:T(8,128)(2,1)} %param.13) | copy-start | bytes 1572868
  2.2 1.2 %copy-start = (f32[1,16,128,128]{3,2,1,0:T(8,128)S(1)}, f32[1,16,128,128]{3,2,1,0:T(8,128)}, u32[]{:S(2)}) copy-start(f32[1,16,128,128]{3,2,1,0:T(8,128)} %param.21) | copy-start | bytes 3145732
  2.2 1.3 %copy-start.1 = (bf16[128,2048]{1,0:T(8,128)(2,1)S(1)}, bf16[128,2048]{1,0:T(8,128)(2,1)}, u32[]{:S(2)}) copy-start(bf16[128,2048]{1,0:T(8,128)(2,1)} %hidden.1) | copy-start | bytes 1572868
  2.3 1.3 %copy-start.2 = (bf16[2048,16]{0,1:T(8,128)(2,1)S(1)}, bf16[2048,16]{0,1:T(8,128)(2,1)}, u32[]{:S(2)}) copy-start(bf16[2048,16]{0,1:T(8,128)(2,1)} %param.16) | copy-start | bytes 196612
  2.3 1.3 %copy-start.3 = (bf16[2048,16]{0,1:T(8,128)(2,1)S(1)}, bf16[2048,16]{0,1:T(8,128)(2,1)}, u32[]{:S(2)}) copy-start(bf16[2048,16]{0,1:T(8,128)(2,1)} %param.17) | copy-start | bytes 196612
  2.6 1.0 %copy-start.4 = (f32[16]{0:T(128)S(1)}, f32[16]{0:T(128)}, u32[]{:S(2)}) copy-start(f32[16]{0:T(128)} %param.18) | copy-start | bytes 196
  2.6 1.0 %copy-start.5 = (f32[16]{0:T(128)S(1)}, f32[16]{0:T(128)}, u32[]{:S(2)}) copy-start(f32[16]{0:T(128)} %param.19) | copy-start | bytes 196
  2.6 1.0 %copy-start.6 = (f32[16]{0:T(128)S(1)}, f32[16]{0:T(128)}, u32[]{:S(2)}) copy-start(f32[16]{0:T(128)} %param.20) | copy-start | bytes 196

commit v3 on v2

--- a/solution.py
+++ b/solution.py
@@ -24,19 +24,37 @@
     return row, col
 
 
-def inverses(couplings):
-    c = couplings[0].shape[0]
+def lockstep(*groups):
+    results = [[None] * len(members) for members, _ in groups]
+    active = {(i, j) for i, (members, _) in enumerate(groups) for j in range(len(members))}
+    tick = 0
+    while active:
+        for i, (members, period) in enumerate(groups):
+            for j, member in enumerate(members):
+                if (i, j) in active and tick % period == 0:
+                    try:
+                        next(member)
+                    except StopIteration as end:
+                        results[i][j] = end.value
+                        active.remove((i, j))
+        tick += 1
+    return results
+
+
+def inverse(a):
+    c = a.shape[0]
     row, col = indices(c)
-    invs = [
-        jnp.where(row == col, 1.0, jnp.where((row ^ col) == 1, -a, 0.0)) for a in couplings
-    ]
+    inv = jnp.where(row == col, 1.0, jnp.where((row ^ col) == 1, -a, 0.0))
     level = 1
     while (2 << level) <= c:
         near = ((row >> level) ^ (col >> level)) == 1
-        halves = [mm(x, jnp.where(near, a, 0.0)) for x, a in zip(invs, couplings)]
-        invs = [x - mm(y, x) for x, y in zip(invs, halves)]
+        half = mm(inv, jnp.where(near, a, 0.0))
+        yield
+        step = mm(half, inv)
+        yield
+        inv = inv - step
         level += 1
-    return invs
+    return inv
 
 
 def head_masks(c):
@@ -60,26 +78,22 @@
     return lax.rsqrt(down(x * x) + EPSILON)
 
 
-def local_first(q, k, rows):
+def local_head(q, k, do, rows):
     c = q.shape[0]
+    dv = do.shape[1]
     eye, upper, strict = head_masks(c)
-    g, beta = rows[0:1], rows[1:2]
+    g, beta, cd, to_end = rows[0:1], rows[1:2], rows[2:3], rows[3:4]
     qt, kt = q.T, k.T
+    grams = mm(k, jnp.concatenate([k, q], axis=0), 1, 1)
+    yield
     rq, rk = scale_of(qt.astype(F32)), scale_of(kt.astype(F32))
     start = to_col(eye, jnp.log(rk) - g)
     decay = jnp.exp(jnp.where(upper, start + g, -1e30))
-    grams = mm(k, jnp.concatenate([k, q], axis=0), 1, 1)
     kk = grams[:, :c]
     pt = decay * rq * grams[:, c:]
     pairs = jnp.where(strict, decay, 0.0) * rk
-    return qt, kt, rq, rk, decay, pairs, kk, pt, beta * pairs * kk
-
-
-def local_map(k, do, rows, inv, first):
-    qt, kt, rq, rk, decay, pairs, kk, pt, a = first
-    beta, cd, to_end = rows[1:2], rows[2:3], rows[3:4]
-    dv = do.shape[1]
     ptdo = mm(pt, do).astype(BF)
+    inv = yield from inverse(beta * pairs * kk)
     left = jnp.concatenate([inv.astype(BF), (inv * (to_end * rk)).astype(BF)], axis=1)
     right = jnp.concatenate(
         [
@@ -89,13 +103,16 @@
         axis=0,
     )
     both = mm(left, right)
+    yield
     left = jnp.concatenate(
         [(qt * (cd * rq)).astype(BF), (kt * (-beta * cd * rk)).astype(BF)], axis=1
     )
     right = jnp.concatenate(
         [jnp.concatenate([do, jnp.zeros(k.shape, BF)], axis=1), both.astype(BF)], axis=0
     )
-    return both[:, :dv], both[:, dv:], mm(left, right)
+    made = mm(left, right)
+    yield
+    return qt, kt, rq, rk, decay, pairs, kk, pt, inv, both[:, :dv], both[:, dv:], made
 
 
 def local_rest(k, v, do, s0, rows, qt, kt, rq, rk, decay, pt, inv):
@@ -105,17 +122,23 @@
     sb = s0.astype(BF)
     ks = mm(k, sb)
     back = inv.T
+    yield
     left = jnp.concatenate([back * beta, back * (-beta * cd * rk)], axis=1)
     ub = mm(left, jnp.concatenate([v, ks.astype(BF)], axis=0)).astype(BF)
+    yield
     prod = mm(jnp.concatenate([ub, sb], axis=0), do, 1, 1)
+    yield
     dpt, dost = prod[:c], prod[c:] * cd
     t = dpt * pt
     gdp = (decay * dpt).astype(BF)
     qn = qt * rq
-    dqn = rq * (dost + mm(kt, gdp))
+    dqk = mm(kt, gdp)
+    dk0 = mm(qn, gdp, 1, 1)
+    yield
+    dg0 = down(t) + down(dost * qn) - to_row(eye, t)
+    dqn = rq * (dost + dqk)
     dq = dqn - qn * down(qn * dqn)
-    dk0 = mm(qn, gdp, 1, 1)
-    dg0 = down(t) + down(dost * qn) - to_row(eye, t)
+    yield
     return dq.astype(BF).T, ks, ub, dk0, dg0
 
 
@@ -124,25 +147,33 @@
     eye, _, _ = head_masks(c)
     beta, cd, to_end = rows[1:2], rows[2:3], rows[3:4]
     w = w0 + mm(nb, e)
+    ue = mm(e, ub, 1, 1)
+    yield
     wb = w.astype(BF)
-    dv = to_col(eye, beta) * w
     prod = mm(jnp.concatenate([ub, s0.astype(BF)], axis=0), wb, 1, 1)
+    ue = (to_end * rk) * ue
+    s = down(kt * ue)
+    wv = to_row(eye, w * v.astype(F32))
+    wks = (cd * rk) * to_row(eye, w * ks)
+    yield
     da = -prod[:c] * pairs
-    ue = (to_end * rk) * mm(e, ub, 1, 1)
     pair = (beta * da).astype(BF)
     kn = kt * rk
-    dkn = dk0 - (beta * cd * rk) * prod[c:] + mm(kt, pair) + mm(kt, pair, 1, 1) + ue
-    dk = dkn - kn * down(kn * dkn)
+    dkn = dk0 - (beta * cd * rk) * prod[c:] + ue
+    near, far = mm(kt, pair), mm(kt, pair, 1, 1)
     da = da * kk
     own = down(da)
-    wks = (cd * rk) * to_row(eye, w * ks)
-    dbeta = own + to_row(eye, w * v.astype(F32)) - wks
-    s = down(kt * ue)
+    dbeta = own + wv - wks
     dg = dg0 + beta * (own - wks) - to_row(eye, beta * da) - s
+    yield
+    dkn = dkn + near + far
+    dk = dkn - kn * down(kn * dkn)
     last = cd[:, c - 1 :]
     tail = jnp.sum(s, keepdims=True) + last * jnp.sum(down(s0 * e.astype(F32)), keepdims=True)
     lane = lax.broadcasted_iota(jnp.int32, (1, c), 1)
     dg = dg + jnp.where(lane == c - 1, tail, 0.0)
+    dv = to_col(eye, beta) * w
+    yield
     return dv, dk.astype(BF).T, dg, dbeta
 
 
@@ -163,11 +194,11 @@
 def whole_kernel(
     n, m, size,
     q, k, v, do, s0, hidden, decay_w, write_w, decay_bias, decay_log, write_bias,
-    dq, dk, dv, gh, gd, gw,
-    rows, fac, weights, qts, kts, scales, decay, pairs, kks, pts, invs, w0, nb, ks, ub, dk0, dg0, dgs, dbs,
-    maps, maps_in, tcomp, bcomp, gcomp, zin, zout, eout, ein,
+    dq_out, dk_out, dv_out, gh, gd, gw,
+    dq, dk, dv, rows, fac, weights, qts, kts, scales, decay, pairs, kks, pts, invs, w0, nb, ks, ub, dk0, dg0, dgs, dbs,
+    ends, ends_in, maps, maps_in, tcomp, bcomp, gcomp, zin, zout, eout, ein,
     tbuf, got, part, gathered, ggot, wgot,
-    map_sems, map_recv, z_sems, e_send, e_recv, sum_sems, head_sems,
+    end_sems, map_sems, map_recv, z_sems, e_send, e_recv, sum_sems, head_sems,
 ):
     me, side = lax.axis_index("seq"), lax.axis_index("head")
     mesh_id = pl.DeviceIdType.MESH
@@ -198,6 +229,20 @@
     def side_behind(d):
         return lax.rem(side + m - d, m)
 
+    def far_first(d):
+        skip = jnp.where(plane < planes // 2, planes - 1 - d // size, d // size)
+        return skip * size + lax.rem(rank + 1 + d, size)
+
+    def to_all(start):
+        def one(d):
+            to = far_first(d)
+
+            @pl.when(to != me)
+            def _():
+                start(to)
+
+        run(0, n, one)
+
     def greet(d):
         pl.semaphore_signal(barrier, inc=1, device_id={"seq": ahead(d)}, device_id_type=mesh_id)
 
@@ -215,6 +260,13 @@
         return pltpu.make_async_remote_copy(
             src_ref=maps.at[b, to], dst_ref=maps_in.at[b, source],
             send_sem=map_sems.at[b, to], recv_sem=map_recv.at[b, source],
+            device_id={"seq": plane * size + to}, device_id_type=mesh_id,
+        )
+
+    def send_ends(to, source):
+        return pltpu.make_async_remote_copy(
+            src_ref=ends, dst_ref=ends_in.at[source],
+            send_sem=end_sems.at[0, to], recv_sem=end_sems.at[1, source],
             device_id={"seq": plane * size + to}, device_id_type=mesh_id,
         )
 
@@ -281,6 +333,8 @@
         fac[:heads] = -rate * jax.nn.sigmoid(pre)
         fac[heads:] = beta * (1.0 - beta)
         parts = (g, beta, jnp.exp(g), jnp.exp(g[:, c - 1 :] - g))
+        ends[...] = jnp.broadcast_to(parts[2][:, c - 1 :], ends.shape)
+        ends_in[rank] = jnp.broadcast_to(parts[2][:, c - 1 :], ends.shape)
         for h in range(heads):
             for i, a in enumerate(parts):
                 rows[h, i : i + 1] = a[h : h + 1]
@@ -288,30 +342,57 @@
     def wait_barrier():
         pl.semaphore_wait(barrier, n + m - 2)
 
-    def local_batch(b):
-        hs = [j * own + b for j in range(size)]
-        firsts = [local_first(q[h], k[h], rows[h]) for h in hs]
-        solved = inverses([first[8] for first in firsts])
-        messages = []
-        for j, h in enumerate(hs):
-            qt, kt, rq, rk, decay_, pairs_, kk, pt, _ = firsts[j]
-            w0_, nb_, made = local_map(k[h], do[h], rows[h], solved[j], firsts[j])
-            qts[h], kts[h] = qt, kt
+    def batch_heads(b):
+        return [j * own + b for j in range(size)]
+
+    def local_parts(b):
+        return [local_head(q[h], k[h], do[h], rows[h]) for h in batch_heads(b)]
+
+    def local_store(b, outs):
+        for j, h in enumerate(batch_heads(b)):
+            qts[h], kts[h], rq, rk, decay[h], pairs[h], kks[h], pts[h], inv, w0_, nb_, made = outs[j]
             scales[h, 0:1] = rq
             scales[h, 1:2] = rk
-            decay[h], pairs[h], kks[h], pts[h] = decay_, pairs_, kk, pt
-            invs[h], w0[h], nb[h] = solved[j].astype(BF), w0_, nb_.astype(BF)
-            last = jnp.broadcast_to(rows[h][2:3, c - 1 :], (8, dvv + dkk))
-            high = last.astype(BF)
-            low = (last - high.astype(F32)).astype(BF)
-            messages.append(jnp.concatenate([made.astype(BF), high, low], axis=0))
-            maps[b, j] = messages[j]
-
+            invs[h], w0[h], nb[h] = inv.astype(BF), w0_, nb_.astype(BF)
+            maps[b, j] = made.astype(BF)
+
+    def rest_parts(b):
+        return [
+            local_rest(
+                k[h], v[h], do[h], s0[h], rows[h], qts[h], kts[h],
+                scales[h, 0:1], scales[h, 1:2], decay[h], pts[h], invs[h],
+            )
+            for h in batch_heads(b)
+        ]
+
+    def rest_store(b, outs):
+        for j, h in enumerate(batch_heads(b)):
+            dq[h], ks[h], ub[h], dk0[h], dg0[h] = outs[j]
+
+    def local_batch(b):
+        local_store(b, lockstep((local_parts(b), 1))[0])
+
+    def rest_batch(b):
+        rest_store(b, lockstep((rest_parts(b), 1))[0])
+
+    def both_batches(s):
+        outs = lockstep((rest_parts(s - 1), 2), (local_parts(s), 1))
+        rest_store(s - 1, outs[0])
+        local_store(s, outs[1])
+
+    def end_sends():
         for j in range(size):
 
-            @pl.when(rank == j)
-            def _():
-                maps_in[b, j] = messages[j]
+            @pl.when(rank != j)
+            def _():
+                send_ends(j, rank).start()
+
+    def wait_ends():
+        for p in range(size):
+
+            @pl.when(rank != p)
+            def _():
+                send_ends(p, p).wait_recv()
 
     def local_sends(b):
         for j in range(size):
@@ -320,10 +401,10 @@
             def _():
                 send_map(b, j, rank).start()
 
+        maps_in[b, rank] = maps[b, rank]
+
     def piece(b, p):
-        made = maps_in[b, p, :dkk]
-        ends = maps_in[b, p, dkk:].astype(F32)
-        return made, ends[0:1] + ends[8:9]
+        return maps_in[b, p], ends_in[p, pl.ds(rank * own + b, 1), :]
 
     def wait_maps(b):
         for p in range(size):
@@ -340,13 +421,13 @@
             made, last = piece(b, p)
             step = made.astype(F32)
             prod = mm(made[:, dvv:], both)
-            both = last * both + jnp.concatenate(
-                [step[:, :dvv], g[:, dvv:] * step[:, dvv:]], axis=1
+            both = last[:, :1] * both + jnp.concatenate(
+                [step[:, :dvv], g[:, :1] * step[:, dvv:]], axis=1
             ) + prod
             g = last * g
         bcomp[b] = both[:, :dvv]
         tcomp[b] = both[:, dvv:].astype(BF)
-        gcomp[b] = jnp.broadcast_to(g[:, :dvv], gcomp.shape[1:])
+        gcomp[b] = jnp.broadcast_to(g, gcomp.shape[1:])
 
     def wait_plane(b):
         @pl.when(lag > 0)
@@ -363,6 +444,8 @@
             zout[b] = e.astype(BF)
             send_plane(b).start()
 
+    def hand_back(b):
+        eb = zin[b]
         e = eb.astype(F32)
         for p in range(size - 1, -1, -1):
             eout[b, p] = eb
@@ -377,16 +460,8 @@
 
             if p > 0:
                 made, last = piece(b, p)
-                e = last[:, :dvv] * e + made[:, :dvv].astype(F32) + mm(made[:, dvv:], eb)
+                e = last * e + made[:, :dvv].astype(F32) + mm(made[:, dvv:], eb)
                 eb = e.astype(BF)
-
-    def rest_batch(b):
-        for j in range(size):
-            h = j * own + b
-            dq[h], ks[h], ub[h], dk0[h], dg0[h] = local_rest(
-                k[h], v[h], do[h], s0[h], rows[h], qts[h], kts[h],
-                scales[h, 0:1], scales[h, 1:2], decay[h], pts[h], invs[h],
-            )
 
     def wait_back(b):
         for j in range(size):
@@ -397,60 +472,76 @@
 
     def carry_batch(b):
         wait_back(b)
-        for j in range(size):
-            h = j * own + b
-            outs = carry_head(
+        parts = [
+            carry_head(
                 v[h], s0[h], ein[h], rows[h], kts[h], scales[h, 1:2], pairs[h], kks[h], ub[h],
                 w0[h], nb[h], ks[h], dk0[h], dg0[h],
             )
-            dv[h] = outs[0].astype(BF)
-            dk[h] = outs[1]
-            dgs[pl.ds(h, 1), :] = outs[2]
-            dbs[pl.ds(h, 1), :] = outs[3]
+            for h in batch_heads(b)
+        ]
+        outs = lockstep((parts, 1))[0]
+        for j, h in enumerate(batch_heads(b)):
+            dv[h] = outs[j][0].astype(BF)
+            dk[h] = outs[j][1]
+            dgs[pl.ds(h, 1), :] = outs[j][2]
+            dbs[pl.ds(h, 1), :] = outs[j][3]
 
     late = max(own, planes) + 1
-    half = (own + 1) // 2
-
-    def step(s):
-        @pl.when(s < own)
-        def _():
-            local_batch(s)
-
-            @pl.when(s == 0)
-            def _():
-                wait_barrier()
-                run(1, m, lambda d: send_weights(side_ahead(d), side).start())
-
-            local_sends(s)
-
+
+    def first_batch():
+        local_batch(0)
+        wait_barrier()
+        run(1, m, lambda d: send_weights(side_ahead(d), side).start())
+        end_sends()
+        local_sends(0)
+
+    def pass_on(s):
         turn = s - 1 - lag
 
         @pl.when((lag > 0) & (turn >= 0) & (turn < own))
         def _():
             hand_on(turn)
 
-        @pl.when(s == own)
-        def _():
-            run(0, half, rest_batch)
-
-        @pl.when((s >= 1) & (s <= own))
-        def _():
-            compose(s - 1)
-
-            @pl.when(lag == 0)
-            def _():
-                hand_on(s - 1)
-
-        @pl.when((s > own) & (s < 2 * own + 1 - half))
-        def _():
-            rest_batch(s - own - 1 + half)
+    def gather_maps(s):
+        @pl.when(s == 1)
+        def _():
+            wait_ends()
+
+        compose(s - 1)
+
+        @pl.when(lag == 0)
+        def _():
+            hand_on(s - 1)
+
+    def early(s):
+        both_batches(s)
+        local_sends(s)
+        pass_on(s)
+        gather_maps(s)
+
+    def middle():
+        pass_on(own)
+        rest_batch(own - 1)
+        gather_maps(own)
+        run(0, jnp.maximum(own - lag, 0), hand_back)
+
+    def later(s):
+        pass_on(s)
+        turn = s - 1 - lag
+
+        @pl.when((turn >= 0) & (turn < own))
+        def _():
+            hand_back(turn)
 
         @pl.when(s >= late)
         def _():
             carry_batch(s - late)
 
     prepare()
-    run(0, own + late, step)
+    first_batch()
+    run(1, own, early)
+    middle()
+    run(own + 1, own + late, later)
 
     def finish_grads():
         row, col = indices(c)
@@ -466,7 +557,7 @@
         terms = mm(grads, hidden[...])
         for i in range(n):
             tbuf[i] = terms[:, i * w : (i + 1) * w].astype(BF)
-        run(1, n, lambda d: scatter(ahead(d), me).start())
+        to_all(lambda to: scatter(to, me).start())
 
     def partner(d):
         source = side_behind(d)
@@ -490,7 +581,7 @@
         acc = lax.fori_loop(1, n, add, tbuf[me].astype(F32)).astype(BF)
         part[...] = acc
         gathered[me] = acc
-        run(1, n, lambda d: gather(ahead(d), me).start())
+        to_all(lambda to: gather(to, me).start())
 
     def arrive(d):
         source = behind(d)
@@ -498,6 +589,10 @@
 
     def arrivals():
         run(1, n, arrive)
+
+    def reorder():
+        for ref, source in ((dq_out, dq), (dk_out, dk), (dv_out, dv)):
+            ref[...] = jnp.swapaxes(source[...], 0, 1)
 
     def write_sums():
         for i in range(n):
@@ -520,8 +615,15 @@
     weight_terms(finish_grads())
     input_grad()
     reduce_terms()
+    reorder()
     arrivals()
     write_sums()
+    for j in range(size):
+
+        @pl.when(rank != j)
+        def _():
+            send_ends(j, rank).wait_send()
+
     run(0, own, done)
     run(1, n, lambda d: scatter(ahead(d), me).wait_send())
     run(1, n, lambda d: gather(ahead(d), me).wait_send())
@@ -538,16 +640,17 @@
     vm = pl.BlockSpec(memory_space=pltpu.VMEM)
     sd = jax.ShapeDtypeStruct
     dma = pltpu.SemaphoreType.DMA
-    message = (dk + 16, dv + dk)
+    message = (dk, dv + dk)
     return pl.pallas_call(
         partial(whole_kernel, n, m, size),
         out_shape=(
-            sd((h, c, dk), BF), sd((h, c, dk), BF), sd((h, c, dv), BF), sd((c, width // m), BF),
+            sd((c, h, dk), BF), sd((c, h, dk), BF), sd((c, h, dv), BF), sd((c, width // m), BF),
             sd((h, width), F32), sd((h, width), F32),
         ),
         in_specs=[vm] * 11,
         out_specs=(vm,) * 6,
         scratch_shapes=[
+            pltpu.VMEM((h, c, dk), BF), pltpu.VMEM((h, c, dk), BF), pltpu.VMEM((h, c, dv), BF),
             pltpu.VMEM((h, 8, c), F32), pltpu.VMEM((2 * h, c), F32),
             pltpu.VMEM((m, 2 * h, width // m), BF),
             pltpu.VMEM((h, dk, c), BF), pltpu.VMEM((h, dk, c), BF), pltpu.VMEM((h, 8, c), F32),
@@ -556,6 +659,7 @@
             pltpu.VMEM((h, c, dk), BF), pltpu.VMEM((h, c, dv), F32), pltpu.VMEM((h, c, dv), BF),
             pltpu.VMEM((h, dk, c), F32),
             pltpu.VMEM((h, 1, c), F32), pltpu.VMEM((h, c), F32), pltpu.VMEM((h, c), F32),
+            pltpu.VMEM((h, dv), F32), pltpu.VMEM((size, h, dv), F32),
             pltpu.VMEM((own, size) + message, BF), pltpu.VMEM((own, size) + message, BF),
             pltpu.VMEM((own, dk, dk), BF), pltpu.VMEM((own, dk, dv), F32),
             pltpu.VMEM((own, 8, dv), F32),
@@ -564,13 +668,37 @@
             pltpu.VMEM((n, 2 * h, width // n), BF), pltpu.VMEM((n, 2 * h, width // n), BF),
             pltpu.VMEM((2 * h, width // n), BF), pltpu.VMEM((n, 2 * h, width // n), BF),
             pltpu.VMEM((m, 2 * h, c), BF), pltpu.VMEM((m, 2 * h, width // m), BF),
-            dma((own, size)), dma((own, size)), dma((2, own)), dma((own, size)), dma((h,)),
+            dma((2, size)), dma((own, size)), dma((own, size)), dma((2, own)), dma((own, size)), dma((h,)),
             dma((4, n)), dma((4, m)),
         ],
         compiler_params=pltpu.CompilerParams(
             collective_id=0, has_side_effects=True, vmem_limit_bytes=28 * 1024 * 1024
         ),
     )(q, k, v, do, s0, hidden, *gates)
+
+
+def store_kernel(*refs):
+    count = (len(refs) - 1) // 2
+    sems = refs[-1]
+    copies = [
+        pltpu.make_async_copy(refs[i], refs[count + i], sems.at[i]) for i in range(count)
+    ]
+    for copy in copies:
+        copy.start()
+    for copy in copies:
+        copy.wait()
+
+
+def store_part(arrays):
+    count = len(arrays)
+    return pl.pallas_call(
+        store_kernel,
+        out_shape=tuple(jax.ShapeDtypeStruct(a.shape, a.dtype) for a in arrays),
+        in_specs=[pl.BlockSpec(memory_space=pltpu.VMEM)] * count,
+        out_specs=(pl.BlockSpec(memory_space=pl.ANY),) * count,
+        scratch_shapes=[pltpu.SemaphoreType.DMA((count,))],
+        compiler_params=pltpu.CompilerParams(vmem_limit_bytes=8 * 1024 * 1024),
+    )(*arrays)
 
 
 def shards(
@@ -588,18 +716,12 @@
 ):
     n, m = lax.axis_size("seq"), lax.axis_size("head")
     q, k, v, do = (jnp.swapaxes(a, 0, 1) for a in (queries, key_vectors, values, out_grad))
-    dq, dk, dv, gh, gd, gw = whole_part(
+    made = whole_part(
         n, m, q, k, v, do, start_state[0], hidden_in, decay_weight.T, write_weight.T,
         decay_bias[None], decay_log[None], write_bias[None],
     )
-    return (
-        jnp.swapaxes(dq, 0, 1),
-        jnp.swapaxes(dk, 0, 1),
-        jnp.swapaxes(dv, 0, 1),
-        gh,
-        gd.T,
-        gw.T,
-    )
+    dq, dk, dv, gh, gd, gw = store_part(made)
+    return dq, dk, dv, gh, gd.T, gw.T
 
 
 def solution(mesh):

time: 63.5 us -> 54.5 us (0.86)
  local copies, waits for them, and re-layouts: 8.29 us -> 2.87 us
  Pallas kernels: 54.3 us -> 50.7 us
    unnamed x24 -> x18, local copies, waits for them, and re-layouts: 6.46 us -> 1.04 us
    pallas_call x1 -> x2, Pallas kernels: 54.3 us -> 50.7 us  [the longest x1 49.3 us: whole_part(): pl.pallas_call(partial(whole_kernel, n, m, size), out_shape=(sd((c, h, dk...]
where the time goes in v3:
time: 54.5 us; the launch traced here: 54.3 us
  Pallas kernels  50.7 us (93%)
  local copies, waits for them, and re-layouts  2.87 us (5%)
  between operations  0.75 us (1%)
    pallas_call x1, Pallas kernels, whole_part(): pl.pallas_call(partial(whole_kernel, n, m, size), out_shape=(sd((c, h, dk...  49.3 us
    transpose x2, local copies, waits for them, and re-layouts, shards(): jnp.swapaxes(a, 0, 1)  1.83 us
    pallas_call x1, Pallas kernels, store_part(): pl.pallas_call(store_kernel, out_shape=tuple((jax.ShapeDtypeStruct(a.shap...  1.36 us

profile of v3, /device:TPU:0, one launch (start us, length us, event | category | flops | bytes accessed | tf_op | source)
XLA Modules:
  0.0 54.3 jit_solution(6824285222444024187)
XLA Ops:
  0.6 0.0 copy-start.7
  0.6 0.0 copy-start.8
  0.7 1.6 %copy_bitcast_fusion.2 = (bf16[16,128,128]{2,1,0:T(8,128)(2,1)S(1)}, bf16[16,128,128]{2,1,0:T(8,128)(2,1)S(1)}) fusion(bf16[128,16,128]{2,1,0:T(8,128)(2,1)} %param.12, bf16[128,16,128]{2,1,0:T(8,128)(2,1)} %param.11), kind=kLoop, calls=%fused_computation.2 | loop fusion | bytes 2097152 | tf_op jit(solution)/shard_map/transpose | solution.py:718
  2.2 0.0 copy-done.7
  2.2 0.0 copy-done.8
  2.2 0.0 copy-start
  2.2 0.0 copy-start.1
  2.3 0.0 copy-start.2
  2.3 0.0 copy-start.3
  2.3 0.3 copy_bitcast_fusion
  2.6 0.0 copy-start.4
  2.6 0.0 copy-start.5
  2.6 0.0 copy-start.6
  2.6 0.9 %copy-done = f32[1,16,128,128]{3,2,1,0:T(8,128)S(1)} copy-done((f32[1,16,128,128]{3,2,1,0:T(8,128)S(1)}, f32[1,16,128,128]{3,2,1,0:T(8,128)}, u32[]{:S(2)}) %copy-start) | copy-done | bytes 1048600
  3.5 0.1 copy-done.1
  3.6 0.0 copy-done.2
  3.6 0.0 copy-done.3
  3.6 0.0 copy-done.4
  3.6 0.0 copy-done.5
  3.6 0.0 copy-done.6
  3.6 49.3 %shard_map.154 = (bf16[128,16,128]{2,1,0:T(8,128)(2,1)S(1)}, bf16[128,16,128]{2,1,0:T(8,128)(2,1)S(1)}, bf16[128,16,128]{2,1,0:T(8,128)(2,1)S(1)}, bf16[128,1024...) custom-call(bf16[16,128,128]{2,1,0:T(8,128)(2,1)S(1)} %get-tuple-element.33.q, ...), custom_call_target="tpu_custom_call" | custom-call | tf_op jit(solution)/shard_map/pallas_call | solution.py:644
  53.0 1.4 %shard_map.155 = (bf16[128,16,128]{2,1,0:T(8,128)(2,1)}, bf16[128,16,128]{2,1,0:T(8,128)(2,1)}, bf16[128,16,128]{2,1,0:T(8,128)(2,1)}, bf16[128,1024]{1,0:T(8,12...) custom-call(bf16[128,16,128]{2,1,0:T(8,128)(2,1)S(1)} %get-tuple-element.18.refs_0_, ...), custom_call_target="tpu_custom_call" | custom-call | tf_op jit(solution)/shard_map/pallas_call | solution.py:694
Async XLA Ops:
  0.6 1.6 %copy-start.7 = (bf16[128,16,128]{2,1,0:T(8,128)(2,1)S(1)}, bf16[128,16,128]{2,1,0:T(8,128)(2,1)}, u32[]{:S(2)}) copy-start(bf16[128,16,128]{2,1,0:T(8,128)(2,1)} %param.14) | copy-start | bytes 1572868
  0.6 1.6 %copy-start.8 = (bf16[128,16,128]{2,1,0:T(8,128)(2,1)S(1)}, bf16[128,16,128]{2,1,0:T(8,128)(2,1)}, u32[]{:S(2)}) copy-start(bf16[128,16,128]{2,1,0:T(8,128)(2,1)} %param.13) | copy-start | bytes 1572868
  2.2 1.2 %copy-start = (f32[1,16,128,128]{3,2,1,0:T(8,128)S(1)}, f32[1,16,128,128]{3,2,1,0:T(8,128)}, u32[]{:S(2)}) copy-start(f32[1,16,128,128]{3,2,1,0:T(8,128)} %param.21) | copy-start | bytes 3145732
  2.2 1.3 %copy-start.1 = (bf16[128,2048]{1,0:T(8,128)(2,1)S(1)}, bf16[128,2048]{1,0:T(8,128)(2,1)}, u32[]{:S(2)}) copy-start(bf16[128,2048]{1,0:T(8,128)(2,1)} %hidden.1) | copy-start | bytes 1572868
  2.3 1.3 %copy-start.2 = (bf16[2048,16]{0,1:T(8,128)(2,1)S(1)}, bf16[2048,16]{0,1:T(8,128)(2,1)}, u32[]{:S(2)}) copy-start(bf16[2048,16]{0,1:T(8,128)(2,1)} %param.16) | copy-start | bytes 196612
  2.3 1.3 %copy-start.3 = (bf16[2048,16]{0,1:T(8,128)(2,1)S(1)}, bf16[2048,16]{0,1:T(8,128)(2,1)}, u32[]{:S(2)}) copy-start(bf16[2048,16]{0,1:T(8,128)(2,1)} %param.17) | copy-start | bytes 196612
  2.6 1.0 %copy-start.4 = (f32[16]{0:T(128)S(1)}, f32[16]{0:T(128)}, u32[]{:S(2)}) copy-start(f32[16]{0:T(128)} %param.18) | copy-start | bytes 196
  2.6 1.0 %copy-start.5 = (f32[16]{0:T(128)S(1)}, f32[16]{0:T(128)}, u32[]{:S(2)}) copy-start(f32[16]{0:T(128)} %param.19) | copy-start | bytes 196
  2.6 1.0 %copy-start.6 = (f32[16]{0:T(128)S(1)}, f32[16]{0:T(128)}, u32[]{:S(2)}) copy-start(f32[16]{0:T(128)} %param.20) | copy-start | bytes 196

commit v4 on v3

--- a/solution.py
+++ b/solution.py
@@ -193,12 +193,14 @@
 
 def whole_kernel(
     n, m, size,
-    q, k, v, do, s0, hidden, decay_w, write_w, decay_bias, decay_log, write_bias,
+    q_in, k_in, v_in, do_in, s0_in, hidden_in, decay_w_in, write_w_in,
+    decay_bias_in, decay_log_in, write_bias_in,
     dq_out, dk_out, dv_out, gh, gd, gw,
-    dq, dk, dv, rows, fac, weights, qts, kts, scales, decay, pairs, kks, pts, invs, w0, nb, ks, ub, dk0, dg0, dgs, dbs,
-    ends, ends_in, maps, maps_in, tcomp, bcomp, gcomp, zin, zout, eout, ein,
+    q_raw, k_raw, v_raw, do_raw, s0, hidden, decay_w, write_w, decay_bias, decay_log, write_bias,
+    q, k, v, do, dq, dk, dv, rows, fac, weights, qts, kts, scales, decay, pairs, kks, pts, invs, w0, nb, ks, ub, dk0, dg0, dgs, dbs,
+    ends, ends_in, maps, maps_in, tcomp, bcomp, gcomp, far_out, far_in, zin, zout, eout, ein,
     tbuf, got, part, gathered, ggot, wgot,
-    end_sems, map_sems, map_recv, z_sems, e_send, e_recv, sum_sems, head_sems,
+    in_sems, far_sems, end_sems, map_sems, map_recv, z_sems, e_send, e_recv, sum_sems, head_sems,
 ):
     me, side = lax.axis_index("seq"), lax.axis_index("head")
     mesh_id = pl.DeviceIdType.MESH
@@ -208,6 +210,8 @@
     planes = n // size
     plane, rank = me // size, lax.rem(me, size)
     lag = planes - 1 - plane
+    direct = min(own, 2)
+    chained = own - direct
     barrier = pltpu.get_barrier_semaphore()
 
     def run(low, high, body):
@@ -250,6 +254,15 @@
         pl.semaphore_signal(
             barrier, inc=1, device_id={"head": side_ahead(d)}, device_id_type=mesh_id
         )
+
+    arrays = (
+        (hidden_in, hidden), (decay_w_in, decay_w), (write_w_in, write_w),
+        (decay_bias_in, decay_bias), (decay_log_in, decay_log), (write_bias_in, write_bias),
+        (k_in, k_raw), (q_in, q_raw), (do_in, do_raw), (v_in, v_raw), (s0_in, s0),
+    )
+    loads = [pltpu.make_async_copy(a, b, in_sems.at[i]) for i, (a, b) in enumerate(arrays)]
+    for load in loads:
+        load.start()
 
     run(1, n, greet)
     run(1, m, greet_side)
@@ -276,6 +289,16 @@
             send_sem=z_sems.at[0, b], recv_sem=z_sems.at[1, b],
             device_id={"seq": lax.rem(me + n - size, n)}, device_id_type=mesh_id,
         )
+
+    def send_far(i, to, source, part):
+        return pltpu.make_async_remote_copy(
+            src_ref=far_out.at[(i,) + part], dst_ref=far_in.at[(i, source) + part],
+            send_sem=far_sems.at[0, i, to], recv_sem=far_sems.at[1, i, source],
+            device_id={"seq": to * size + rank}, device_id_type=mesh_id,
+        )
+
+    whole_map = (pl.ds(0, dkk + 16), pl.ds(0, dvv + dkk))
+    offset_only = (pl.ds(0, dkk), pl.ds(0, dvv))
 
     def send_back(b, to, owner):
         return pltpu.make_async_remote_copy(
@@ -444,6 +467,38 @@
             zout[b] = e.astype(BF)
             send_plane(b).start()
 
+    def send_fars(b):
+        i = b - chained
+        g = gcomp[b]
+        high = g.astype(BF)
+        low = (g - high.astype(F32)).astype(BF)
+        far_out[i, :dkk] = jnp.concatenate([bcomp[b].astype(BF), tcomp[b]], axis=1)
+        far_out[i, dkk : dkk + 8, :dvv] = high
+        far_out[i, dkk + 8 :, :dvv] = low
+
+        @pl.when(lag == 0)
+        def _():
+            run(0, plane, lambda p: send_far(i, p, plane, offset_only).start())
+
+        @pl.when(lag > 0)
+        def _():
+            run(0, plane, lambda p: send_far(i, p, plane, whole_map).start())
+
+    def resolve(b):
+        i = b - chained
+        send_far(i, planes - 1, planes - 1, offset_only).wait_recv()
+
+        def fold(d, e):
+            source = planes - 2 - d
+            send_far(i, source, source, whole_map).wait_recv()
+            made = far_in[i, source, :dkk]
+            g = far_in[i, source, dkk:, :dvv].astype(F32)
+            prod = mm(made[:, dvv:], e)
+            return (g[0:1] + g[8:9]) * e + made[:, :dvv].astype(F32) + prod
+
+        e = far_in[i, planes - 1, :dkk, :dvv].astype(F32)
+        zin[b] = lax.fori_loop(0, lag - 1, fold, e).astype(BF)
+
     def hand_back(b):
         eb = zin[b]
         e = eb.astype(F32)
@@ -488,6 +543,7 @@
 
     late = max(own, planes) + 1
 
+
     def first_batch():
         local_batch(0)
         wait_barrier()
@@ -498,9 +554,13 @@
     def pass_on(s):
         turn = s - 1 - lag
 
-        @pl.when((lag > 0) & (turn >= 0) & (turn < own))
+        @pl.when((lag > 0) & (turn >= 0) & (turn < chained))
         def _():
             hand_on(turn)
+
+        @pl.when((lag > 0) & (turn >= chained) & (turn < own))
+        def _():
+            resolve(turn)
 
     def gather_maps(s):
         @pl.when(s == 1)
@@ -509,9 +569,13 @@
 
         compose(s - 1)
 
-        @pl.when(lag == 0)
+        @pl.when((lag == 0) & (s <= chained))
         def _():
             hand_on(s - 1)
+
+        @pl.when((plane > 0) & (s > chained))
+        def _():
+            send_fars(s - 1)
 
     def early(s):
         both_batches(s)
@@ -537,8 +601,17 @@
         def _():
             carry_batch(s - late)
 
+    def take(first, last, pairs):
+        for load in loads[first:last]:
+            load.wait()
+        for ref, raw in pairs:
+            ref[...] = jnp.swapaxes(raw[...], 0, 1)
+
+    take(0, 6, ())
     prepare()
+    take(6, 9, ((k, k_raw), (q, q_raw), (do, do_raw)))
     first_batch()
+    take(9, 11, ((v, v_raw),))
     run(1, own, early)
     middle()
     run(own + 1, own + late, later)
@@ -608,9 +681,17 @@
                 send_map(b, j, rank).wait_send()
                 send_back(b, j, rank).wait_send()
 
-        @pl.when(plane > 0)
+        @pl.when((plane > 0) & (b < chained))
         def _():
             send_plane(b).wait_send()
+
+        @pl.when((b >= chained) & (lag == 0))
+        def _():
+            run(0, plane, lambda p: send_far(b - chained, p, plane, offset_only).wait_send())
+
+        @pl.when((b >= chained) & (lag > 0))
+        def _():
+            run(0, plane, lambda p: send_far(b - chained, p, plane, whole_map).wait_send())
 
     weight_terms(finish_grads())
     input_grad()
@@ -632,7 +713,7 @@
 
 
 def whole_part(n, m, q, k, v, do, s0, hidden, *gates):
-    h, c, dk = q.shape
+    c, h, dk = q.shape
     dv = v.shape[2]
     size = group_size(n, h)
     own = h // size
@@ -644,12 +725,15 @@
     return pl.pallas_call(
         partial(whole_kernel, n, m, size),
         out_shape=(
-            sd((c, h, dk), BF), sd((c, h, dk), BF), sd((c, h, dv), BF), sd((c, width // m), BF),
-            sd((h, width), F32), sd((h, width), F32),
+            pltpu.VMEM((c, h, dk), BF), pltpu.VMEM((c, h, dk), BF), pltpu.VMEM((c, h, dv), BF), pltpu.VMEM((c, width // m), BF),
+            pltpu.VMEM((h, width), F32), pltpu.VMEM((h, width), F32),
         ),
-        in_specs=[vm] * 11,
+        in_specs=[pl.BlockSpec(memory_space=pl.ANY)] * 11,
         out_specs=(vm,) * 6,
-        scratch_shapes=[
+        scratch_shapes=[pltpu.VMEM(a.shape, a.dtype) for a in (q, k, v, do, s0, hidden) + gates]
+        + [
+            pltpu.VMEM((h, c, dk), BF), pltpu.VMEM((h, c, dk), BF), pltpu.VMEM((h, c, dv), BF),
+            pltpu.VMEM((h, c, dv), BF),
             pltpu.VMEM((h, c, dk), BF), pltpu.VMEM((h, c, dk), BF), pltpu.VMEM((h, c, dv), BF),
             pltpu.VMEM((h, 8, c), F32), pltpu.VMEM((2 * h, c), F32),
             pltpu.VMEM((m, 2 * h, width // m), BF),
@@ -663,16 +747,18 @@
             pltpu.VMEM((own, size) + message, BF), pltpu.VMEM((own, size) + message, BF),
             pltpu.VMEM((own, dk, dk), BF), pltpu.VMEM((own, dk, dv), F32),
             pltpu.VMEM((own, 8, dv), F32),
+            pltpu.VMEM((min(own, 2), dk + 16, dv + dk), BF),
+            pltpu.VMEM((min(own, 2), n // size, dk + 16, dv + dk), BF),
             pltpu.VMEM((own, dk, dv), BF), pltpu.VMEM((own, dk, dv), BF),
             pltpu.VMEM((own, size, dk, dv), BF), pltpu.VMEM((h, dk, dv), BF),
             pltpu.VMEM((n, 2 * h, width // n), BF), pltpu.VMEM((n, 2 * h, width // n), BF),
             pltpu.VMEM((2 * h, width // n), BF), pltpu.VMEM((n, 2 * h, width // n), BF),
             pltpu.VMEM((m, 2 * h, c), BF), pltpu.VMEM((m, 2 * h, width // m), BF),
-            dma((2, size)), dma((own, size)), dma((own, size)), dma((2, own)), dma((own, size)), dma((h,)),
+            dma((11,)), dma((2, min(own, 2), n // size)), dma((2, size)), dma((own, size)), dma((own, size)), dma((2, own)), dma((own, size)), dma((h,)),
             dma((4, n)), dma((4, m)),
         ],
         compiler_params=pltpu.CompilerParams(
-            collective_id=0, has_side_effects=True, vmem_limit_bytes=28 * 1024 * 1024
+            collective_id=0, has_side_effects=True, vmem_limit_bytes=57000 * 1024
         ),
     )(q, k, v, do, s0, hidden, *gates)
 
@@ -715,9 +801,8 @@
     start_state,
 ):
     n, m = lax.axis_size("seq"), lax.axis_size("head")
-    q, k, v, do = (jnp.swapaxes(a, 0, 1) for a in (queries, key_vectors, values, out_grad))
     made = whole_part(
-        n, m, q, k, v, do, start_state[0], hidden_in, decay_weight.T, write_weight.T,
+        n, m, queries, key_vectors, values, out_grad, start_state[0], hidden_in, decay_weight.T, write_weight.T,
         decay_bias[None], decay_log[None], write_bias[None],
     )
     dq, dk, dv, gh, gd, gw = store_part(made)

time: 54.5 us -> 51.8 us (0.950)
  local copies, waits for them, and re-layouts: 2.87 us -> 0 us
    transpose x2 -> x0, local copies, waits for them, and re-layouts: 1.83 us -> none  [shards(): jnp.swapaxes(a, 0, 1)]
    unnamed x18 -> x0, local copies, waits for them, and re-layouts: 1.04 us -> none
where the time goes in v4:
time: 51.8 us; the launch traced here: 51.7 us
  Pallas kernels  51 us (98%)
  between operations  0.64 us (1%)
    pallas_call x1, Pallas kernels, whole_part(): pl.pallas_call(partial(whole_kernel, n, m, size), out_shape=(pltpu.VMEM((...  49.7 us
    pallas_call x1, Pallas kernels, store_part(): pl.pallas_call(store_kernel, out_shape=tuple((jax.ShapeDtypeStruct(a.shap...  1.36 us

profile of v4, /device:TPU:0, one launch (start us, length us, event | category | flops | bytes accessed | tf_op | source)
XLA Modules:
  0.0 51.7 jit_solution(7861842922686306043)
XLA Ops:
  0.6 49.7 %shard_map.154 = (bf16[128,16,128]{2,1,0:T(8,128)(2,1)S(1)}, bf16[128,16,128]{2,1,0:T(8,128)(2,1)S(1)}, bf16[128,16,128]{2,1,0:T(8,128)(2,1)S(1)}, bf16[128,1024...) custom-call(bf16[128,16,128]{2,1,0:T(8,128)(2,1)} %q_in.1, bf16[128,16,128]{2,1,0:T(8,128)(2,1)} %k_in.1, ...), custom_call_target="tpu_custom_call" | custom-call | tf_op jit(solution)/shard_map/pallas_call | solution.py:725
  50.3 1.4 %shard_map.155 = (bf16[128,16,128]{2,1,0:T(8,128)(2,1)}, bf16[128,16,128]{2,1,0:T(8,128)(2,1)}, bf16[128,16,128]{2,1,0:T(8,128)(2,1)}, bf16[128,1024]{1,0:T(8,12...) custom-call(bf16[128,16,128]{2,1,0:T(8,128)(2,1)S(1)} %get-tuple-element.18.refs_0_, ...), custom_call_target="tpu_custom_call" | custom-call | tf_op jit(solution)/shard_map/pallas_call | solution.py:780

commit v5 on v4

--- a/solution.py
+++ b/solution.py
@@ -189,6 +189,11 @@
     while (2 * size) ** 2 <= n and heads % (2 * size) == 0 and n % (2 * size) == 0:
         size *= 2
     return size
+
+
+def middle_planes(planes):
+    low = planes // 4
+    return low, planes - 2 * low
 
 
 def whole_kernel(
@@ -267,7 +272,11 @@
     run(1, n, greet)
     run(1, m, greet_side)
     width = hidden.shape[1]
-    w = width // n
+    low, count = middle_planes(planes)
+    base, adders = low * size, count * size
+    w = width // adders
+    seat = me - base
+    adding = (seat >= 0) & (seat < adders)
 
     def send_map(b, to, source):
         return pltpu.make_async_remote_copy(
@@ -311,7 +320,7 @@
         return pltpu.make_async_remote_copy(
             src_ref=tbuf.at[to], dst_ref=got.at[source],
             send_sem=sum_sems.at[0, to], recv_sem=sum_sems.at[1, source],
-            device_id={"seq": to}, device_id_type=mesh_id,
+            device_id={"seq": base + to}, device_id_type=mesh_id,
         )
 
     def gather(to, source):
@@ -438,50 +447,69 @@
 
     def compose(b):
         wait_maps(b)
-        made, g = piece(b, size - 1)
-        both = made.astype(F32)
-        for p in range(size - 2, -1, -1):
-            made, last = piece(b, p)
-            step = made.astype(F32)
-            prod = mm(made[:, dvv:], both)
-            both = last[:, :1] * both + jnp.concatenate(
-                [step[:, :dvv], g[:, :1] * step[:, dvv:]], axis=1
-            ) + prod
-            g = last * g
-        bcomp[b] = both[:, :dvv]
-        tcomp[b] = both[:, dvv:].astype(BF)
-        gcomp[b] = jnp.broadcast_to(g, gcomp.shape[1:])
+        @pl.when(lag == 0)
+        def _():
+            both = maps_in[b, size - 1, :, :dvv].astype(F32)
+            for p in range(size - 2, -1, -1):
+                made, last = piece(b, p)
+                prod = mm(made[:, dvv:], both)
+                both = last[:, :1] * both + made[:, :dvv].astype(F32) + prod
+            bcomp[b] = both
+
+        @pl.when((lag > 0) & (plane > 0))
+        def _():
+            made, g = piece(b, size - 1)
+            both = made.astype(F32)
+            for p in range(size - 2, -1, -1):
+                made, last = piece(b, p)
+                step = made.astype(F32)
+                prod = mm(made[:, dvv:], both)
+                both = last[:, :1] * both + jnp.concatenate(
+                    [step[:, :dvv], g[:, :1] * step[:, dvv:]], axis=1
+                ) + prod
+                g = last * g
+            bcomp[b] = both[:, :dvv]
+            tcomp[b] = both[:, dvv:].astype(BF)
+            gcomp[b] = jnp.broadcast_to(g, gcomp.shape[1:])
 
     def wait_plane(b):
+        send_plane(b).wait_recv()
+
+    def hand_on(b):
+        @pl.when((lag == 0) & (plane > 0))
+        def _():
+            zout[b] = bcomp[b].astype(BF)
+
         @pl.when(lag > 0)
         def _():
-            send_plane(b).wait_recv()
-
-    def hand_on(b):
-        wait_plane(b)
-        eb = zin[b]
+            wait_plane(b)
+
+            @pl.when(plane > 0)
+            def _():
+                eb = zin[b]
+                e = gcomp[b, 0:1] * eb.astype(F32) + bcomp[b] + mm(tcomp[b], eb)
+                zout[b] = e.astype(BF)
 
         @pl.when(plane > 0)
         def _():
-            e = gcomp[b, 0:1] * eb.astype(F32) + bcomp[b] + mm(tcomp[b], eb)
-            zout[b] = e.astype(BF)
             send_plane(b).start()
 
     def send_fars(b):
         i = b - chained
-        g = gcomp[b]
-        high = g.astype(BF)
-        low = (g - high.astype(F32)).astype(BF)
-        far_out[i, :dkk] = jnp.concatenate([bcomp[b].astype(BF), tcomp[b]], axis=1)
-        far_out[i, dkk : dkk + 8, :dvv] = high
-        far_out[i, dkk + 8 :, :dvv] = low
 
         @pl.when(lag == 0)
         def _():
+            far_out[i, :dkk, :dvv] = bcomp[b].astype(BF)
             run(0, plane, lambda p: send_far(i, p, plane, offset_only).start())
 
         @pl.when(lag > 0)
         def _():
+            g = gcomp[b]
+            high = g.astype(BF)
+            low = (g - high.astype(F32)).astype(BF)
+            far_out[i, :dkk] = jnp.concatenate([bcomp[b].astype(BF), tcomp[b]], axis=1)
+            far_out[i, dkk : dkk + 8, :dvv] = high
+            far_out[i, dkk + 8 :, :dvv] = low
             run(0, plane, lambda p: send_far(i, p, plane, whole_map).start())
 
     def resolve(b):
@@ -541,7 +569,7 @@
             dgs[pl.ds(h, 1), :] = outs[j][2]
             dbs[pl.ds(h, 1), :] = outs[j][3]
 
-    late = max(own, planes) + 1
+    late = max(own, planes) + 2
 
 
     def first_batch():
@@ -628,9 +656,15 @@
 
     def weight_terms(grads):
         terms = mm(grads, hidden[...])
-        for i in range(n):
+        for i in range(adders):
             tbuf[i] = terms[:, i * w : (i + 1) * w].astype(BF)
-        to_all(lambda to: scatter(to, me).start())
+
+        def give(to):
+            @pl.when((to >= base) & (to < base + adders))
+            def _():
+                scatter(to - base, me).start()
+
+        to_all(give)
 
     def partner(d):
         source = side_behind(d)
@@ -648,27 +682,30 @@
     def reduce_terms():
         def add(d, acc):
             source = behind(d)
-            scatter(source, source).wait_recv()
+            scatter(seat, source).wait_recv()
             return acc + got[source].astype(F32)
 
-        acc = lax.fori_loop(1, n, add, tbuf[me].astype(F32)).astype(BF)
-        part[...] = acc
-        gathered[me] = acc
-        to_all(lambda to: gather(to, me).start())
-
-    def arrive(d):
-        source = behind(d)
-        gather(source, source).wait_recv()
+        @pl.when(adding)
+        def _():
+            acc = lax.fori_loop(1, n, add, tbuf[seat].astype(F32)).astype(BF)
+            part[...] = acc
+            gathered[seat] = acc
+            to_all(lambda to: gather(to, seat).start())
 
     def arrivals():
-        run(1, n, arrive)
+        def arrive(i):
+            @pl.when(i != seat)
+            def _():
+                gather(base, i).wait_recv()
+
+        run(0, adders, arrive)
 
     def reorder():
         for ref, source in ((dq_out, dq), (dk_out, dk), (dv_out, dv)):
             ref[...] = jnp.swapaxes(source[...], 0, 1)
 
     def write_sums():
-        for i in range(n):
+        for i in range(adders):
             both = gathered[i].astype(F32)
             gd[:, i * w : (i + 1) * w] = both[:heads]
             gw[:, i * w : (i + 1) * w] = both[heads:]
@@ -706,8 +743,17 @@
             send_ends(j, rank).wait_send()
 
     run(0, own, done)
-    run(1, n, lambda d: scatter(ahead(d), me).wait_send())
-    run(1, n, lambda d: gather(ahead(d), me).wait_send())
+    def given(i):
+        @pl.when(i != seat)
+        def _():
+            scatter(i, me).wait_send()
+
+    run(0, adders, given)
+
+    @pl.when(adding)
+    def _():
+        run(1, n, lambda d: gather(ahead(d), seat).wait_send())
+
     run(1, m, lambda d: send_weights(side_ahead(d), side).wait_send())
     run(1, m, lambda d: send_grads(side_ahead(d), side).wait_send())
 
@@ -718,6 +764,8 @@
     size = group_size(n, h)
     own = h // size
     width = hidden.shape[1]
+    adders = middle_planes(n // size)[1] * size
+    w = width // adders
     vm = pl.BlockSpec(memory_space=pltpu.VMEM)
     sd = jax.ShapeDtypeStruct
     dma = pltpu.SemaphoreType.DMA
@@ -751,8 +799,8 @@
             pltpu.VMEM((min(own, 2), n // size, dk + 16, dv + dk), BF),
             pltpu.VMEM((own, dk, dv), BF), pltpu.VMEM((own, dk, dv), BF),
             pltpu.VMEM((own, size, dk, dv), BF), pltpu.VMEM((h, dk, dv), BF),
-            pltpu.VMEM((n, 2 * h, width // n), BF), pltpu.VMEM((n, 2 * h, width // n), BF),
-            pltpu.VMEM((2 * h, width // n), BF), pltpu.VMEM((n, 2 * h, width // n), BF),
+            pltpu.VMEM((adders, 2 * h, w), BF), pltpu.VMEM((n, 2 * h, w), BF),
+            pltpu.VMEM((2 * h, w), BF), pltpu.VMEM((adders, 2 * h, w), BF),
             pltpu.VMEM((m, 2 * h, c), BF), pltpu.VMEM((m, 2 * h, width // m), BF),
             dma((11,)), dma((2, min(own, 2), n // size)), dma((2, size)), dma((own, size)), dma((own, size)), dma((2, own)), dma((own, size)), dma((h,)),
             dma((4, n)), dma((4, m)),

time: 51.8 us -> 49.8 us (0.961)
  Pallas kernels: 51 us -> 49 us
    pallas_call x1, Pallas kernels: 49.7 us -> 47.6 us  [whole_part(): pl.pallas_call(partial(whole_kernel, n, m, size), out_shape=(pltpu.VMEM((...]
where the time goes in v5:
time: 49.8 us; the launch traced here: 49.6 us
  Pallas kernels  49 us (98%)
  between operations  0.64 us (1%)
    pallas_call x1, Pallas kernels, whole_part(): pl.pallas_call(partial(whole_kernel, n, m, size), out_shape=(pltpu.VMEM((...  47.6 us
    pallas_call x1, Pallas kernels, store_part(): pl.pallas_call(store_kernel, out_shape=tuple((jax.ShapeDtypeStruct(a.shap...  1.36 us

profile of v5, /device:TPU:0, one launch (start us, length us, event | category | flops | bytes accessed | tf_op | source)
XLA Modules:
  0.0 49.6 jit_solution(12928539078486519185)
XLA Ops:
  0.6 47.6 %shard_map.154 = (bf16[128,16,128]{2,1,0:T(8,128)(2,1)S(1)}, bf16[128,16,128]{2,1,0:T(8,128)(2,1)S(1)}, bf16[128,16,128]{2,1,0:T(8,128)(2,1)S(1)}, bf16[128,1024...) custom-call(bf16[128,16,128]{2,1,0:T(8,128)(2,1)} %q_in.1, bf16[128,16,128]{2,1,0:T(8,128)(2,1)} %k_in.1, ...), custom_call_target="tpu_custom_call" | custom-call | tf_op jit(solution)/shard_map/pallas_call | solution.py:773
  48.3 1.4 %shard_map.155 = (bf16[128,16,128]{2,1,0:T(8,128)(2,1)}, bf16[128,16,128]{2,1,0:T(8,128)(2,1)}, bf16[128,16,128]{2,1,0:T(8,128)(2,1)}, bf16[128,1024]{1,0:T(8,12...) custom-call(bf16[128,16,128]{2,1,0:T(8,128)(2,1)S(1)} %get-tuple-element.18.refs_0_, ...), custom_call_target="tpu_custom_call" | custom-call | tf_op jit(solution)/shard_map/pallas_call | solution.py:828

commit v6 on v5

--- a/solution.py
+++ b/solution.py
@@ -609,12 +609,16 @@
         both_batches(s)
         local_sends(s)
         pass_on(s)
-        gather_maps(s)
+        turn = jnp.where(lag == 0, s - 1, s)
+
+        @pl.when(turn > 0)
+        def _():
+            gather_maps(turn)
 
     def middle():
         pass_on(own)
         rest_batch(own - 1)
-        gather_maps(own)
+        run(jnp.where(lag == 0, max(own - 1, 1), own), own + 1, gather_maps)
         run(0, jnp.maximum(own - lag, 0), hand_back)
 
     def later(s):

time: 49.8 us -> 49.5 us (level)
  no operation moved by 1% of the time
where the time goes in v6:
time: 49.5 us; the launch traced here: 49.4 us
  Pallas kernels  48.7 us (98%)
  between operations  0.64 us (1%)
    pallas_call x1, Pallas kernels, whole_part(): pl.pallas_call(partial(whole_kernel, n, m, size), out_shape=(pltpu.VMEM((...  47.4 us
    pallas_call x1, Pallas kernels, store_part(): pl.pallas_call(store_kernel, out_shape=tuple((jax.ShapeDtypeStruct(a.shap...  1.36 us

profile of v6, /device:TPU:0, one launch (start us, length us, event | category | flops | bytes accessed | tf_op | source)
XLA Modules:
  0.0 49.4 jit_solution(13567944275566742012)
XLA Ops:
  0.6 47.4 %shard_map.154 = (bf16[128,16,128]{2,1,0:T(8,128)(2,1)S(1)}, bf16[128,16,128]{2,1,0:T(8,128)(2,1)S(1)}, bf16[128,16,128]{2,1,0:T(8,128)(2,1)S(1)}, bf16[128,1024...) custom-call(bf16[128,16,128]{2,1,0:T(8,128)(2,1)} %q_in.1, bf16[128,16,128]{2,1,0:T(8,128)(2,1)} %k_in.1, ...), custom_call_target="tpu_custom_call" | custom-call | tf_op jit(solution)/shard_map/pallas_call | solution.py:777
  48.0 1.4 %shard_map.155 = (bf16[128,16,128]{2,1,0:T(8,128)(2,1)}, bf16[128,16,128]{2,1,0:T(8,128)(2,1)}, bf16[128,16,128]{2,1,0:T(8,128)(2,1)}, bf16[128,1024]{1,0:T(8,12...) custom-call(bf16[128,16,128]{2,1,0:T(8,128)(2,1)S(1)} %get-tuple-element.18.refs_0_, ...), custom_call_target="tpu_custom_call" | custom-call | tf_op jit(solution)/shard_map/pallas_call | solution.py:832
